TPU v7x, 32 devices: a whole 2x2x4 slice. The times are simulated.
32 devices in a mesh: row: 4 (over x, core), col: 8 (over z, y).
Axes of the slice: x: 2, y: 2, z: 4, core: 2. Of those that a mesh axis runs over, the one named last changes fastest.
Arguments:
- velocity_start: float32 [2, 256, 1024], P(None, 'row', 'col'), may hold values from -3 to 3
- stress_start: float32 [3, 256, 1024], P(None, 'row', 'col'), may hold values from -3 to 3
- wind_stress: float32 [2, 256, 1024], P(None, 'row', 'col'), may hold values from -6 to 6
- ocean_current: float32 [2, 256, 1024], P(None, 'row', 'col'), may hold values from -3 to 3
- ice_area: float32 [5, 256, 1024], P(None, 'row', 'col'), may hold values from 0.15 to 0.2
- ice_volume: float32 [5, 256, 1024], P(None, 'row', 'col'), may hold values from 0.05 to 0.6
- inverse_width: float32 [256, 1024], P('row', 'col'), may hold values from 0.7 to 1.4
- inverse_height: float32 [256, 1024], P('row', 'col'), may hold values from 0.7 to 1.4
- land_block: int32 [64, 32], P('row', 'col'), may hold values 0 or 1
- ice_block: int32 [64, 32], P('row', 'col'), may hold values 0 or 1
- writer: int32 [8], replicated, may hold values from 0 to 3
Outputs:
- velocity: float32 [2, 256, 1024], P(None, 'row', 'col')
- stress: float32 [3, 256, 1024], P(None, 'row', 'col')
- restart: float32 [4, 10, 256, 1024], P('row', None, None, 'col')
All inputs are finite; a program needn't handle non-finite values. No bound on the sum of `land_block` or of `ice_block` on one device may be relied on, other than what follows from the above.
Results may differ from a plain program's by a relative error of at most 0.00002.
Values sent between devices are 32-bit elements; how exact they have to be, the bound alone decides.
A program may use at most 64 MiB of HBM per device.

v0:
```python
import jax
import jax.numpy as jnp
from jax import lax
from jax.sharding import PartitionSpec as P

SUB = 12


strength_scale = 4.0
hibler_decay = 20.0
mass_rate = 16.0
water_drag = 1.0
coriolis = 0.5
relax_rate = 0.5
ellipse_square = 4.0
delta_margin = 0.5


def shifted(value, axis, steps):
    count = lax.axis_size(axis)
    pairs = [(source, (source + steps) % count) for source in range(count)]
    return lax.ppermute(value, axis, pairs)


def from_behind(value, axis, by):
    count = lax.axis_size(axis)
    pairs = [(i, i + by) for i in range(count) if 0 <= i + by < count]
    return lax.ppermute(value, axis, pairs)


def partner(value, axis, stride):
    return lax.ppermute(value, axis, [(i, i ^ 1 << stride) for i in range(lax.axis_size(axis))])


def extended(value, sides, width):
    for axis, dim in sides:
        count, length = (lax.axis_size(axis), value.shape[dim])
        up = [(i, (i + 1) % count) for i in range(count)]
        down = [(j, i) for i, j in up]
        last = lax.slice_in_dim(value, length - width, length, axis=dim)
        first = lax.slice_in_dim(value, 0, width, axis=dim)
        before = lax.ppermute(last, axis, up)
        after = lax.ppermute(first, axis, down)
        value = jnp.concatenate([before, value, after], axis=dim)
    return value


def expand_blocks(blocks, height, breadth):
    counted = blocks.astype(jnp.float32)
    block_rows, block_cols = counted.shape
    spread = jnp.broadcast_to(
        counted[:, None, :, None],
        (block_rows, height // block_rows, block_cols, breadth // block_cols),
    )
    return spread.reshape(height, breadth)


def stress_update(
    stresses, strength, across_scale, along_scale, north_east, north_west, south_east, south_west
):
    grad_ux = 0.5 * across_scale * (north_east[0] + south_east[0] - (north_west[0] + south_west[0]))
    grad_vy = 0.5 * along_scale * (north_east[1] + north_west[1] - (south_east[1] + south_west[1]))
    grad_uy = 0.5 * along_scale * (north_east[0] + north_west[0] - (south_east[0] + south_west[0]))
    grad_vx = 0.5 * across_scale * (north_east[1] + south_east[1] - (north_west[1] + south_west[1]))
    divergence = grad_ux + grad_vy
    tension = grad_ux - grad_vy
    shearing = grad_uy + grad_vx
    deform = jnp.sqrt(
        divergence * divergence + (tension * tension + shearing * shearing) / ellipse_square
    )
    viscous = strength / (deform + delta_margin)
    normal_sum = (stresses[0] + relax_rate * viscous * (divergence - deform)) / (1.0 + relax_rate)
    normal_diff = (stresses[1] + relax_rate * viscous * tension / ellipse_square) / (
        1.0 + relax_rate
    )
    shear_new = (stresses[2] + relax_rate * viscous * shearing / (2.0 * ellipse_square)) / (
        1.0 + relax_rate
    )
    return jnp.stack([normal_sum, normal_diff, shear_new])


def normal_xx(stresses):
    return 0.5 * (stresses[0] + stresses[1])


def normal_yy(stresses):
    return 0.5 * (stresses[0] - stresses[1])


def stress_force(across_scale, along_scale, south_west, south_east, north_west, north_east):
    force_x = 0.5 * across_scale * (
        normal_xx(south_east)
        + normal_xx(north_east)
        - (normal_xx(south_west) + normal_xx(north_west))
    ) + 0.5 * along_scale * (north_west[2] + north_east[2] - (south_west[2] + south_east[2]))
    force_y = 0.5 * across_scale * (
        south_east[2] + north_east[2] - (south_west[2] + north_west[2])
    ) + 0.5 * along_scale * (
        normal_yy(north_west)
        + normal_yy(north_east)
        - (normal_yy(south_west) + normal_yy(south_east))
    )
    return (force_x, force_y)


def momentum(
    velocity, force_x, force_y, inertia, turning, wind_stress, ocean_current, land_cells, ice_cells
):
    damped = inertia + water_drag
    right_x = inertia * velocity[0] + force_x + wind_stress[0] + water_drag * ocean_current[0]
    right_y = inertia * velocity[1] + force_y + wind_stress[1] + water_drag * ocean_current[1]
    denominator = damped * damped + turning * turning
    next_u = (damped * right_x + turning * right_y) / denominator
    next_v = (damped * right_y - turning * right_x) / denominator
    moving = jnp.stack([next_u, next_v])
    return land_cells * (ice_cells * moving + (1.0 - ice_cells) * ocean_current)


def neighbour_views(stacked, offset):
    members = stacked.shape[0]
    edge_line = stacked[:, :, 0]
    arrived = shifted(edge_line, "col", offset)
    beside = jnp.concatenate([stacked[:, :, 1:], arrived[:, :, None]], axis=2)
    rows_out = jnp.concatenate([stacked[:, 0], beside[:, 0]], axis=0)
    landed = from_behind(rows_out, "row", offset)
    vertical = jnp.concatenate([stacked[:, 1:], landed[:members, None]], axis=1)
    diagonal = jnp.concatenate([beside[:, 1:], landed[members:, None]], axis=1)
    return (beside, vertical, diagonal)


def fold_ghost(stresses):
    top_row = stresses[:, -1, :]
    edge_value = shifted(top_row[:, -1:], "col", 1)
    packed = jnp.concatenate([top_row, edge_value], axis=1)
    for bit in range(lax.axis_size("col").bit_length() - 1):
        packed = partner(packed, "col", bit)
    return jnp.concatenate([packed[:, :-1][:, ::-1], packed[:, -1:]], axis=1)


def widen_block(own_cells, east_side, north_side, north_east):
    lower = jnp.concatenate([own_cells, east_side[:, :, -1:]], axis=2)
    upper = jnp.concatenate([north_side[:, -1:], north_east[:, -1:, -1:]], axis=2)
    return jnp.concatenate([lower, upper], axis=1)


def restart_strip(ice_area, ice_volume, writer):
    snapshot = jnp.concatenate([ice_area, ice_volume], axis=0)
    strip_rows = lax.all_gather(snapshot, "row", axis=1, tiled=True)
    strips = jnp.arange(writer.shape[0], dtype=jnp.int32)
    chosen = jnp.sum(jnp.where(strips == lax.axis_index("col"), writer, 0))
    is_writer = chosen == lax.axis_index("row")
    return jnp.where(is_writer, strip_rows, jnp.zeros_like(strip_rows))[None]


def shards(
    velocity_start,
    stress_start,
    wind_stress,
    ocean_current,
    ice_area,
    ice_volume,
    inverse_width,
    inverse_height,
    land_block,
    ice_block,
    writer,
):
    height, breadth = inverse_width.shape
    land_cells = expand_blocks(land_block, height, breadth)
    ice_cells = expand_blocks(ice_block, height, breadth)
    area_total = jnp.sum(ice_area, axis=0)
    volume_total = jnp.sum(ice_volume, axis=0)
    strength = (
        strength_scale * volume_total * jnp.exp(-hibler_decay * (1.0 - area_total)) * land_cells
    )
    inertia = mass_rate * (1.0 + volume_total)
    turning = coriolis * (1.0 + volume_total)
    is_top = lax.axis_index("row") == lax.axis_size("row") - 1
    is_bottom = lax.axis_index("row") == 0
    statics = jnp.concatenate(
        [stress_start, strength[None], inverse_width[None], inverse_height[None]], axis=0
    )
    east_side, north_side, north_east = neighbour_views(statics, -1)
    widened = widen_block(statics, east_side, north_side, north_east)
    strength_wide = widened[3]
    width_wide = widened[4]
    height_wide = widened[5]

    def recompute_cycle(subcycle, carried):
        velocity, stress_wide = carried
        padded = extended(velocity, (("row", 1), ("col", 2)), 1)
        padded = padded.at[:, 0].set(jnp.where(is_bottom, 0.0, padded[:, 0]))
        stress_wide = stress_update(
            stress_wide,
            strength_wide,
            width_wide,
            height_wide,
            padded[:, 1:, 1:],
            padded[:, 1:, :-1],
            padded[:, :-1, 1:],
            padded[:, :-1, :-1],
        )
        ghost_row = fold_ghost(stress_wide[:, :-1, :-1])
        stress_wide = stress_wide.at[:, -1].set(jnp.where(is_top, ghost_row, stress_wide[:, -1]))
        force_x, force_y = stress_force(
            inverse_width,
            inverse_height,
            stress_wide[:, :-1, :-1],
            stress_wide[:, :-1, 1:],
            stress_wide[:, 1:, :-1],
            stress_wide[:, 1:, 1:],
        )
        velocity = momentum(
            velocity,
            force_x,
            force_y,
            inertia,
            turning,
            wind_stress,
            ocean_current,
            land_cells,
            ice_cells,
        )
        return (velocity, stress_wide)

    velocity, stress_wide = lax.fori_loop(0, SUB, recompute_cycle, (velocity_start, widened[:3]))
    stresses = stress_wide[:, :-1, :-1]
    restart = restart_strip(ice_area, ice_volume, writer)
    return (velocity, stresses, restart)


def solution(mesh):
    return jax.shard_map(
        shards,
        mesh=mesh,
        in_specs=(
            P(None, "row", "col"),
            P(None, "row", "col"),
            P(None, "row", "col"),
            P(None, "row", "col"),
            P(None, "row", "col"),
            P(None, "row", "col"),
            P("row", "col"),
            P("row", "col"),
            P("row", "col"),
            P("row", "col"),
            P(),
        ),
        out_specs=(P(None, "row", "col"), P(None, "row", "col"), P("row", None, None, "col")),
        check_vma=False,
    )
```

profile of v0, /device:TPU:0, one launch (start us, length us, event | category | flops | bytes accessed | tf_op | source)
XLA Modules:
  0.0 391.2 jit_solution(12845675867024995508)
XLA Ops:
  11.3 6.1 %collective-permute-start.8 = (f32[6,64]{1,0:T(8,128)S(1)}, f32[6,64]{1,0:T(8,128)S(1)}, u32[]{:S(2)}, u32[]{:S(2)}) collective-permute-start(f32[6,64]{1,0:T(8,128)S(1)} %bitcast.134), channel_id=1, source_target_pairs={{0,7},{1,0},{2,1},{3,2},{4,3},{5,4},{6,5},{7,6},{8,15},{9,8},{10,9... | collective-permute-start | bytes 4616 | tf_op jit(solution)/shard_map/ppermute | solution.py:22
  22.5 360.1 %while.19 = (s32[]{:T(128)}, f32[2,64,128]{2,1,0:T(8,128)S(1)}, f32[3,65,129]{2,1,0:T(8,128)S(1)}, f32[64,128]{1,0:T(8,128)S(1)}, f32[64,128]{1,0:T(8,128)S(1)},...) while((s32[]{:T(128)}, f32[2,64,128]{2,1,0:T(8,128)S(1)}, ...), condition=%wide.region_3.0_spmd.clone.clone, body=%wide.region_2.3_spmd.clone.clone.sunk | while | flops 1131050 | bytes 3020059 | solution.py:226
  27.9 5.0 %collective-permute-start.2 = (f32[2,66,1]{2,1,0:T(8,128)S(1)}, f32[2,66,1]{2,1,0:T(8,128)S(1)}, u32[]{:S(2)}, u32[]{:S(2)}) collective-permute-start(f32[2,66,1]{2,1,0:T(8,128)S(1)} %get-tuple-element.703), channel_id=1, source_target_pairs={{1,0},{2,1},{3,2},{4,3},{5,4},{6,5},{7,6},{0,7},{9,8},{10,9},{11,1... | collective-permute-start | bytes 1592 | tf_op jit(solution)/shard_map/while/body/eval_jaxpr/ppermute | solution.py:43
  35.0 5.1 %collective-permute-done.3 = f32[2,66,1]{2,1,0:T(8,128)S(1)} collective-permute-done((f32[2,66,1]{2,1,0:T(8,128)S(1)}, f32[2,66,1]{2,1,0:T(8,128)S(1)}, u32[]{:S(2)}, u32[]{:S(2)}) %collective-permute-start.3) | collective-permute-done | bytes 560 | tf_op jit(solution)/shard_map/while/body/eval_jaxpr/ppermute | solution.py:42
  40.6 6.3 %collective-permute-done.4 = f32[3,1]{1,0:T(4,128)S(1)} collective-permute-done((f32[3,1]{1,0:T(4,128)S(1)}, f32[3,1]{1,0:T(4,128)S(1)}, u32[]{:S(2)}, u32[]{:S(2)}) %collective-permute-start.4) | collective-permute-done | bytes 44 | tf_op jit(solution)/shard_map/while/body/eval_jaxpr/ppermute | solution.py:22
  46.9 3.6 collective-permute-done.5
  50.7 3.4 collective-permute-done.6
  54.4 4.3 %collective-permute-done.7 = f32[3,129]{1,0:T(4,128)S(1)} collective-permute-done((f32[3,129]{1,0:T(4,128)S(1)}, f32[3,129]{1,0:T(4,128)S(1)}, u32[]{:S(2)}, u32[]{:S(2)}) %collective-permute-start.7) | collective-permute-done | bytes 1580 | tf_op jit(solution)/shard_map/while/body/eval_jaxpr/ppermute | solution.py:32
  66.7 2.8 collective-permute-done.3
  70.1 6.3 %collective-permute-done.4 = f32[3,1]{1,0:T(4,128)S(1)} collective-permute-done((f32[3,1]{1,0:T(4,128)S(1)}, f32[3,1]{1,0:T(4,128)S(1)}, u32[]{:S(2)}, u32[]{:S(2)}) %collective-permute-start.4) | collective-permute-done | bytes 44 | tf_op jit(solution)/shard_map/while/body/eval_jaxpr/ppermute | solution.py:22
  76.3 3.6 collective-permute-done.5
  80.2 3.4 collective-permute-done.6
  83.8 4.3 %collective-permute-done.7 = f32[3,129]{1,0:T(4,128)S(1)} collective-permute-done((f32[3,129]{1,0:T(4,128)S(1)}, f32[3,129]{1,0:T(4,128)S(1)}, u32[]{:S(2)}, u32[]{:S(2)}) %collective-permute-start.7) | collective-permute-done | bytes 1580 | tf_op jit(solution)/shard_map/while/body/eval_jaxpr/ppermute | solution.py:32
  93.9 2.2 collective-permute-done.2
  96.1 2.8 collective-permute-done.3
  99.5 6.3 %collective-permute-done.4 = f32[3,1]{1,0:T(4,128)S(1)} collective-permute-done((f32[3,1]{1,0:T(4,128)S(1)}, f32[3,1]{1,0:T(4,128)S(1)}, u32[]{:S(2)}, u32[]{:S(2)}) %collective-permute-start.4) | collective-permute-done | bytes 44 | tf_op jit(solution)/shard_map/while/body/eval_jaxpr/ppermute | solution.py:22
  105.8 3.6 collective-permute-done.5
  109.6 3.4 collective-permute-done.6
  113.2 4.3 %collective-permute-done.7 = f32[3,129]{1,0:T(4,128)S(1)} collective-permute-done((f32[3,129]{1,0:T(4,128)S(1)}, f32[3,129]{1,0:T(4,128)S(1)}, u32[]{:S(2)}, u32[]{:S(2)}) %collective-permute-start.7) | collective-permute-done | bytes 1580 | tf_op jit(solution)/shard_map/while/body/eval_jaxpr/ppermute | solution.py:32
  125.5 2.8 collective-permute-done.3
  128.9 6.3 %collective-permute-done.4 = f32[3,1]{1,0:T(4,128)S(1)} collective-permute-done((f32[3,1]{1,0:T(4,128)S(1)}, f32[3,1]{1,0:T(4,128)S(1)}, u32[]{:S(2)}, u32[]{:S(2)}) %collective-permute-start.4) | collective-permute-done | bytes 44 | tf_op jit(solution)/shard_map/while/body/eval_jaxpr/ppermute | solution.py:22
  135.2 3.6 collective-permute-done.5
  139.0 3.4 collective-permute-done.6
  142.6 4.3 %collective-permute-done.7 = f32[3,129]{1,0:T(4,128)S(1)} collective-permute-done((f32[3,129]{1,0:T(4,128)S(1)}, f32[3,129]{1,0:T(4,128)S(1)}, u32[]{:S(2)}, u32[]{:S(2)}) %collective-permute-start.7) | collective-permute-done | bytes 1580 | tf_op jit(solution)/shard_map/while/body/eval_jaxpr/ppermute | solution.py:32
  154.9 2.8 collective-permute-done.3
  158.3 6.3 %collective-permute-done.4 = f32[3,1]{1,0:T(4,128)S(1)} collective-permute-done((f32[3,1]{1,0:T(4,128)S(1)}, f32[3,1]{1,0:T(4,128)S(1)}, u32[]{:S(2)}, u32[]{:S(2)}) %collective-permute-start.4) | collective-permute-done | bytes 44 | tf_op jit(solution)/shard_map/while/body/eval_jaxpr/ppermute | solution.py:22
  164.6 3.6 collective-permute-done.5
  168.4 3.4 collective-permute-done.6
  172.0 4.3 %collective-permute-done.7 = f32[3,129]{1,0:T(4,128)S(1)} collective-permute-done((f32[3,129]{1,0:T(4,128)S(1)}, f32[3,129]{1,0:T(4,128)S(1)}, u32[]{:S(2)}, u32[]{:S(2)}) %collective-permute-start.7) | collective-permute-done | bytes 1580 | tf_op jit(solution)/shard_map/while/body/eval_jaxpr/ppermute | solution.py:32
  184.3 2.8 collective-permute-done.3
  187.7 6.3 %collective-permute-done.4 = f32[3,1]{1,0:T(4,128)S(1)} collective-permute-done((f32[3,1]{1,0:T(4,128)S(1)}, f32[3,1]{1,0:T(4,128)S(1)}, u32[]{:S(2)}, u32[]{:S(2)}) %collective-permute-start.4) | collective-permute-done | bytes 44 | tf_op jit(solution)/shard_map/while/body/eval_jaxpr/ppermute | solution.py:22
  194.0 3.6 collective-permute-done.5
  197.8 3.4 collective-permute-done.6
  201.4 4.3 %collective-permute-done.7 = f32[3,129]{1,0:T(4,128)S(1)} collective-permute-done((f32[3,129]{1,0:T(4,128)S(1)}, f32[3,129]{1,0:T(4,128)S(1)}, u32[]{:S(2)}, u32[]{:S(2)}) %collective-permute-start.7) | collective-permute-done | bytes 1580 | tf_op jit(solution)/shard_map/while/body/eval_jaxpr/ppermute | solution.py:32
  213.7 2.8 collective-permute-done.3
  217.1 6.3 %collective-permute-done.4 = f32[3,1]{1,0:T(4,128)S(1)} collective-permute-done((f32[3,1]{1,0:T(4,128)S(1)}, f32[3,1]{1,0:T(4,128)S(1)}, u32[]{:S(2)}, u32[]{:S(2)}) %collective-permute-start.4) | collective-permute-done | bytes 44 | tf_op jit(solution)/shard_map/while/body/eval_jaxpr/ppermute | solution.py:22
  223.4 3.6 collective-permute-done.5
  227.2 3.4 collective-permute-done.6
  230.8 4.3 %collective-permute-done.7 = f32[3,129]{1,0:T(4,128)S(1)} collective-permute-done((f32[3,129]{1,0:T(4,128)S(1)}, f32[3,129]{1,0:T(4,128)S(1)}, u32[]{:S(2)}, u32[]{:S(2)}) %collective-permute-start.7) | collective-permute-done | bytes 1580 | tf_op jit(solution)/shard_map/while/body/eval_jaxpr/ppermute | solution.py:32
  243.1 2.8 collective-permute-done.3
  246.5 6.3 %collective-permute-done.4 = f32[3,1]{1,0:T(4,128)S(1)} collective-permute-done((f32[3,1]{1,0:T(4,128)S(1)}, f32[3,1]{1,0:T(4,128)S(1)}, u32[]{:S(2)}, u32[]{:S(2)}) %collective-permute-start.4) | collective-permute-done | bytes 44 | tf_op jit(solution)/shard_map/while/body/eval_jaxpr/ppermute | solution.py:22
  252.8 3.6 collective-permute-done.5
  256.6 3.4 collective-permute-done.6
  260.2 4.3 %collective-permute-done.7 = f32[3,129]{1,0:T(4,128)S(1)} collective-permute-done((f32[3,129]{1,0:T(4,128)S(1)}, f32[3,129]{1,0:T(4,128)S(1)}, u32[]{:S(2)}, u32[]{:S(2)}) %collective-permute-start.7) | collective-permute-done | bytes 1580 | tf_op jit(solution)/shard_map/while/body/eval_jaxpr/ppermute | solution.py:32
  272.5 2.8 collective-permute-done.3
  275.9 6.3 %collective-permute-done.4 = f32[3,1]{1,0:T(4,128)S(1)} collective-permute-done((f32[3,1]{1,0:T(4,128)S(1)}, f32[3,1]{1,0:T(4,128)S(1)}, u32[]{:S(2)}, u32[]{:S(2)}) %collective-permute-start.4) | collective-permute-done | bytes 44 | tf_op jit(solution)/shard_map/while/body/eval_jaxpr/ppermute | solution.py:22
  282.2 3.6 collective-permute-done.5
  286.0 3.4 collective-permute-done.6
  289.6 4.3 %collective-permute-done.7 = f32[3,129]{1,0:T(4,128)S(1)} collective-permute-done((f32[3,129]{1,0:T(4,128)S(1)}, f32[3,129]{1,0:T(4,128)S(1)}, u32[]{:S(2)}, u32[]{:S(2)}) %collective-permute-start.7) | collective-permute-done | bytes 1580 | tf_op jit(solution)/shard_map/while/body/eval_jaxpr/ppermute | solution.py:32
  301.9 2.8 collective-permute-done.3
  305.3 6.3 %collective-permute-done.4 = f32[3,1]{1,0:T(4,128)S(1)} collective-permute-done((f32[3,1]{1,0:T(4,128)S(1)}, f32[3,1]{1,0:T(4,128)S(1)}, u32[]{:S(2)}, u32[]{:S(2)}) %collective-permute-start.4) | collective-permute-done | bytes 44 | tf_op jit(solution)/shard_map/while/body/eval_jaxpr/ppermute | solution.py:22
  311.6 3.6 collective-permute-done.5
  315.4 3.4 collective-permute-done.6
  319.0 4.3 %collective-permute-done.7 = f32[3,129]{1,0:T(4,128)S(1)} collective-permute-done((f32[3,129]{1,0:T(4,128)S(1)}, f32[3,129]{1,0:T(4,128)S(1)}, u32[]{:S(2)}, u32[]{:S(2)}) %collective-permute-start.7) | collective-permute-done | bytes 1580 | tf_op jit(solution)/shard_map/while/body/eval_jaxpr/ppermute | solution.py:32
  331.3 2.8 collective-permute-done.3
  334.7 6.3 %collective-permute-done.4 = f32[3,1]{1,0:T(4,128)S(1)} collective-permute-done((f32[3,1]{1,0:T(4,128)S(1)}, f32[3,1]{1,0:T(4,128)S(1)}, u32[]{:S(2)}, u32[]{:S(2)}) %collective-permute-start.4) | collective-permute-done | bytes 44 | tf_op jit(solution)/shard_map/while/body/eval_jaxpr/ppermute | solution.py:22
  341.0 3.6 collective-permute-done.5
  344.8 3.4 collective-permute-done.6
  348.4 4.3 %collective-permute-done.7 = f32[3,129]{1,0:T(4,128)S(1)} collective-permute-done((f32[3,129]{1,0:T(4,128)S(1)}, f32[3,129]{1,0:T(4,128)S(1)}, u32[]{:S(2)}, u32[]{:S(2)}) %collective-permute-start.7) | collective-permute-done | bytes 1580 | tf_op jit(solution)/shard_map/while/body/eval_jaxpr/ppermute | solution.py:32
  360.8 2.8 collective-permute-done.3
  364.1 6.3 %collective-permute-done.4 = f32[3,1]{1,0:T(4,128)S(1)} collective-permute-done((f32[3,1]{1,0:T(4,128)S(1)}, f32[3,1]{1,0:T(4,128)S(1)}, u32[]{:S(2)}, u32[]{:S(2)}) %collective-permute-start.4) | collective-permute-done | bytes 44 | tf_op jit(solution)/shard_map/while/body/eval_jaxpr/ppermute | solution.py:22
  370.4 3.6 collective-permute-done.5
  374.2 3.4 collective-permute-done.6
  377.9 4.3 %collective-permute-done.7 = f32[3,129]{1,0:T(4,128)S(1)} collective-permute-done((f32[3,129]{1,0:T(4,128)S(1)}, f32[3,129]{1,0:T(4,128)S(1)}, u32[]{:S(2)}, u32[]{:S(2)}) %collective-permute-start.7) | collective-permute-done | bytes 1580 | tf_op jit(solution)/shard_map/while/body/eval_jaxpr/ppermute | solution.py:32
  (526 shorter events, 115.0 us)
Async XLA Ops:
  7.2 376.0 %all-gather.2.cloned.1.call-start = ((), (), s32[]{:S(2)}) async-start(), calls=%async_computation | async-start | bytes 1638400 | tf_op jit(solution)/shard_map/all_gather | solution.py:148
  11.3 7.4 %collective-permute-start.8 = (f32[6,64]{1,0:T(8,128)S(1)}, f32[6,64]{1,0:T(8,128)S(1)}, u32[]{:S(2)}, u32[]{:S(2)}) collective-permute-start(f32[6,64]{1,0:T(8,128)S(1)} %bitcast.134), channel_id=1, source_target_pairs={{0,7},{1,0},{2,1},{3,2},{4,3},{5,4},{6,5},{7,6},{8,15},{9,8},{10,9... | collective-permute-start | bytes 4616 | tf_op jit(solution)/shard_map/ppermute | solution.py:22
  27.9 7.0 %collective-permute-start.2 = (f32[2,66,1]{2,1,0:T(8,128)S(1)}, f32[2,66,1]{2,1,0:T(8,128)S(1)}, u32[]{:S(2)}, u32[]{:S(2)}) collective-permute-start(f32[2,66,1]{2,1,0:T(8,128)S(1)} %get-tuple-element.703), channel_id=1, source_target_pairs={{1,0},{2,1},{3,2},{4,3},{5,4},{6,5},{7,6},{0,7},{9,8},{10,9},{11,1... | collective-permute-start | bytes 1592 | tf_op jit(solution)/shard_map/while/body/eval_jaxpr/ppermute | solution.py:43
  33.0 7.0 %collective-permute-start.3 = (f32[2,66,1]{2,1,0:T(8,128)S(1)}, f32[2,66,1]{2,1,0:T(8,128)S(1)}, u32[]{:S(2)}, u32[]{:S(2)}) collective-permute-start(f32[2,66,1]{2,1,0:T(8,128)S(1)} %get-tuple-element.704), channel_id=1, source_target_pairs={{0,1},{1,2},{2,3},{3,4},{4,5},{5,6},{6,7},{7,0},{8,9},{9,10},{10,1... | collective-permute-start | bytes 1592 | tf_op jit(solution)/shard_map/while/body/eval_jaxpr/ppermute | solution.py:42
  40.6 6.3 %collective-permute-start.4 = (f32[3,1]{1,0:T(4,128)S(1)}, f32[3,1]{1,0:T(4,128)S(1)}, u32[]{:S(2)}, u32[]{:S(2)}) collective-permute-start(f32[3,1]{1,0:T(4,128)S(1)} %slice.651), channel_id=1, source_target_pairs={{0,1},{1,2},{2,3},{3,4},{4,5},{5,6},{6,7},{7,0},{8,9},{9,10},{10,1... | collective-permute-start | bytes 44 | tf_op jit(solution)/shard_map/while/body/eval_jaxpr/ppermute | solution.py:22
  46.9 3.6 collective-permute-start.5
  50.5 3.6 collective-permute-start.6
  54.1 4.5 %collective-permute-start.7 = (f32[3,129]{1,0:T(4,128)S(1)}, f32[3,129]{1,0:T(4,128)S(1)}, u32[]{:S(2)}, u32[]{:S(2)}) collective-permute-start(f32[3,129]{1,0:T(4,128)S(1)} %collective-permute-done.6), channel_id=1, source_target_pairs={{0,4},{1,5},{2,6},{3,7},{4,0},{5,1},{6,2},{7,3},{8,12},{9,13},{10,... | collective-permute-start | bytes 4652 | tf_op jit(solution)/shard_map/while/body/eval_jaxpr/ppermute | solution.py:32
  62.3 4.4 %collective-permute-start.2 = (f32[2,66,1]{2,1,0:T(8,128)S(1)}, f32[2,66,1]{2,1,0:T(8,128)S(1)}, u32[]{:S(2)}, u32[]{:S(2)}) collective-permute-start(f32[2,66,1]{2,1,0:T(8,128)S(1)} %get-tuple-element.703), channel_id=1, source_target_pairs={{1,0},{2,1},{3,2},{4,3},{5,4},{6,5},{7,6},{0,7},{9,8},{10,9},{11,1... | collective-permute-start | bytes 1592 | tf_op jit(solution)/shard_map/while/body/eval_jaxpr/ppermute | solution.py:43
  62.3 7.1 %collective-permute-start.3 = (f32[2,66,1]{2,1,0:T(8,128)S(1)}, f32[2,66,1]{2,1,0:T(8,128)S(1)}, u32[]{:S(2)}, u32[]{:S(2)}) collective-permute-start(f32[2,66,1]{2,1,0:T(8,128)S(1)} %get-tuple-element.704), channel_id=1, source_target_pairs={{0,1},{1,2},{2,3},{3,4},{4,5},{5,6},{6,7},{7,0},{8,9},{9,10},{10,1... | collective-permute-start | bytes 1592 | tf_op jit(solution)/shard_map/while/body/eval_jaxpr/ppermute | solution.py:42
  70.0 6.3 %collective-permute-start.4 = (f32[3,1]{1,0:T(4,128)S(1)}, f32[3,1]{1,0:T(4,128)S(1)}, u32[]{:S(2)}, u32[]{:S(2)}) collective-permute-start(f32[3,1]{1,0:T(4,128)S(1)} %slice.651), channel_id=1, source_target_pairs={{0,1},{1,2},{2,3},{3,4},{4,5},{5,6},{6,7},{7,0},{8,9},{9,10},{10,1... | collective-permute-start | bytes 44 | tf_op jit(solution)/shard_map/while/body/eval_jaxpr/ppermute | solution.py:22
  76.3 3.6 collective-permute-start.5
  79.9 3.6 collective-permute-start.6
  83.6 4.5 %collective-permute-start.7 = (f32[3,129]{1,0:T(4,128)S(1)}, f32[3,129]{1,0:T(4,128)S(1)}, u32[]{:S(2)}, u32[]{:S(2)}) collective-permute-start(f32[3,129]{1,0:T(4,128)S(1)} %collective-permute-done.6), channel_id=1, source_target_pairs={{0,4},{1,5},{2,6},{3,7},{4,0},{5,1},{6,2},{7,3},{8,12},{9,13},{10,... | collective-permute-start | bytes 4652 | tf_op jit(solution)/shard_map/while/body/eval_jaxpr/ppermute | solution.py:32
  91.7 4.4 %collective-permute-start.2 = (f32[2,66,1]{2,1,0:T(8,128)S(1)}, f32[2,66,1]{2,1,0:T(8,128)S(1)}, u32[]{:S(2)}, u32[]{:S(2)}) collective-permute-start(f32[2,66,1]{2,1,0:T(8,128)S(1)} %get-tuple-element.703), channel_id=1, source_target_pairs={{1,0},{2,1},{3,2},{4,3},{5,4},{6,5},{7,6},{0,7},{9,8},{10,9},{11,1... | collective-permute-start | bytes 1592 | tf_op jit(solution)/shard_map/while/body/eval_jaxpr/ppermute | solution.py:43
  91.7 7.1 %collective-permute-start.3 = (f32[2,66,1]{2,1,0:T(8,128)S(1)}, f32[2,66,1]{2,1,0:T(8,128)S(1)}, u32[]{:S(2)}, u32[]{:S(2)}) collective-permute-start(f32[2,66,1]{2,1,0:T(8,128)S(1)} %get-tuple-element.704), channel_id=1, source_target_pairs={{0,1},{1,2},{2,3},{3,4},{4,5},{5,6},{6,7},{7,0},{8,9},{9,10},{10,1... | collective-permute-start | bytes 1592 | tf_op jit(solution)/shard_map/while/body/eval_jaxpr/ppermute | solution.py:42
  99.5 6.3 %collective-permute-start.4 = (f32[3,1]{1,0:T(4,128)S(1)}, f32[3,1]{1,0:T(4,128)S(1)}, u32[]{:S(2)}, u32[]{:S(2)}) collective-permute-start(f32[3,1]{1,0:T(4,128)S(1)} %slice.651), channel_id=1, source_target_pairs={{0,1},{1,2},{2,3},{3,4},{4,5},{5,6},{6,7},{7,0},{8,9},{9,10},{10,1... | collective-permute-start | bytes 44 | tf_op jit(solution)/shard_map/while/body/eval_jaxpr/ppermute | solution.py:22
  105.7 3.6 collective-permute-start.5
  109.4 3.6 collective-permute-start.6
  113.0 4.5 %collective-permute-start.7 = (f32[3,129]{1,0:T(4,128)S(1)}, f32[3,129]{1,0:T(4,128)S(1)}, u32[]{:S(2)}, u32[]{:S(2)}) collective-permute-start(f32[3,129]{1,0:T(4,128)S(1)} %collective-permute-done.6), channel_id=1, source_target_pairs={{0,4},{1,5},{2,6},{3,7},{4,0},{5,1},{6,2},{7,3},{8,12},{9,13},{10,... | collective-permute-start | bytes 4652 | tf_op jit(solution)/shard_map/while/body/eval_jaxpr/ppermute | solution.py:32
  121.1 4.4 %collective-permute-start.2 = (f32[2,66,1]{2,1,0:T(8,128)S(1)}, f32[2,66,1]{2,1,0:T(8,128)S(1)}, u32[]{:S(2)}, u32[]{:S(2)}) collective-permute-start(f32[2,66,1]{2,1,0:T(8,128)S(1)} %get-tuple-element.703), channel_id=1, source_target_pairs={{1,0},{2,1},{3,2},{4,3},{5,4},{6,5},{7,6},{0,7},{9,8},{10,9},{11,1... | collective-permute-start | bytes 1592 | tf_op jit(solution)/shard_map/while/body/eval_jaxpr/ppermute | solution.py:43
  121.1 7.1 %collective-permute-start.3 = (f32[2,66,1]{2,1,0:T(8,128)S(1)}, f32[2,66,1]{2,1,0:T(8,128)S(1)}, u32[]{:S(2)}, u32[]{:S(2)}) collective-permute-start(f32[2,66,1]{2,1,0:T(8,128)S(1)} %get-tuple-element.704), channel_id=1, source_target_pairs={{0,1},{1,2},{2,3},{3,4},{4,5},{5,6},{6,7},{7,0},{8,9},{9,10},{10,1... | collective-permute-start | bytes 1592 | tf_op jit(solution)/shard_map/while/body/eval_jaxpr/ppermute | solution.py:42
  128.9 6.3 %collective-permute-start.4 = (f32[3,1]{1,0:T(4,128)S(1)}, f32[3,1]{1,0:T(4,128)S(1)}, u32[]{:S(2)}, u32[]{:S(2)}) collective-permute-start(f32[3,1]{1,0:T(4,128)S(1)} %slice.651), channel_id=1, source_target_pairs={{0,1},{1,2},{2,3},{3,4},{4,5},{5,6},{6,7},{7,0},{8,9},{9,10},{10,1... | collective-permute-start | bytes 44 | tf_op jit(solution)/shard_map/while/body/eval_jaxpr/ppermute | solution.py:22
  135.2 3.6 collective-permute-start.5
  138.8 3.6 collective-permute-start.6
  142.4 4.5 %collective-permute-start.7 = (f32[3,129]{1,0:T(4,128)S(1)}, f32[3,129]{1,0:T(4,128)S(1)}, u32[]{:S(2)}, u32[]{:S(2)}) collective-permute-start(f32[3,129]{1,0:T(4,128)S(1)} %collective-permute-done.6), channel_id=1, source_target_pairs={{0,4},{1,5},{2,6},{3,7},{4,0},{5,1},{6,2},{7,3},{8,12},{9,13},{10,... | collective-permute-start | bytes 4652 | tf_op jit(solution)/shard_map/while/body/eval_jaxpr/ppermute | solution.py:32
  150.5 4.4 %collective-permute-start.2 = (f32[2,66,1]{2,1,0:T(8,128)S(1)}, f32[2,66,1]{2,1,0:T(8,128)S(1)}, u32[]{:S(2)}, u32[]{:S(2)}) collective-permute-start(f32[2,66,1]{2,1,0:T(8,128)S(1)} %get-tuple-element.703), channel_id=1, source_target_pairs={{1,0},{2,1},{3,2},{4,3},{5,4},{6,5},{7,6},{0,7},{9,8},{10,9},{11,1... | collective-permute-start | bytes 1592 | tf_op jit(solution)/shard_map/while/body/eval_jaxpr/ppermute | solution.py:43
  150.6 7.1 %collective-permute-start.3 = (f32[2,66,1]{2,1,0:T(8,128)S(1)}, f32[2,66,1]{2,1,0:T(8,128)S(1)}, u32[]{:S(2)}, u32[]{:S(2)}) collective-permute-start(f32[2,66,1]{2,1,0:T(8,128)S(1)} %get-tuple-element.704), channel_id=1, source_target_pairs={{0,1},{1,2},{2,3},{3,4},{4,5},{5,6},{6,7},{7,0},{8,9},{9,10},{10,1... | collective-permute-start | bytes 1592 | tf_op jit(solution)/shard_map/while/body/eval_jaxpr/ppermute | solution.py:42
  158.3 6.3 %collective-permute-start.4 = (f32[3,1]{1,0:T(4,128)S(1)}, f32[3,1]{1,0:T(4,128)S(1)}, u32[]{:S(2)}, u32[]{:S(2)}) collective-permute-start(f32[3,1]{1,0:T(4,128)S(1)} %slice.651), channel_id=1, source_target_pairs={{0,1},{1,2},{2,3},{3,4},{4,5},{5,6},{6,7},{7,0},{8,9},{9,10},{10,1... | collective-permute-start | bytes 44 | tf_op jit(solution)/shard_map/while/body/eval_jaxpr/ppermute | solution.py:22
  164.6 3.6 collective-permute-start.5
  171.8 4.5 %collective-permute-start.7 = (f32[3,129]{1,0:T(4,128)S(1)}, f32[3,129]{1,0:T(4,128)S(1)}, u32[]{:S(2)}, u32[]{:S(2)}) collective-permute-start(f32[3,129]{1,0:T(4,128)S(1)} %collective-permute-done.6), channel_id=1, source_target_pairs={{0,4},{1,5},{2,6},{3,7},{4,0},{5,1},{6,2},{7,3},{8,12},{9,13},{10,... | collective-permute-start | bytes 4652 | tf_op jit(solution)/shard_map/while/body/eval_jaxpr/ppermute | solution.py:32
  179.9 4.4 %collective-permute-start.2 = (f32[2,66,1]{2,1,0:T(8,128)S(1)}, f32[2,66,1]{2,1,0:T(8,128)S(1)}, u32[]{:S(2)}, u32[]{:S(2)}) collective-permute-start(f32[2,66,1]{2,1,0:T(8,128)S(1)} %get-tuple-element.703), channel_id=1, source_target_pairs={{1,0},{2,1},{3,2},{4,3},{5,4},{6,5},{7,6},{0,7},{9,8},{10,9},{11,1... | collective-permute-start | bytes 1592 | tf_op jit(solution)/shard_map/while/body/eval_jaxpr/ppermute | solution.py:43
  180.0 7.1 %collective-permute-start.3 = (f32[2,66,1]{2,1,0:T(8,128)S(1)}, f32[2,66,1]{2,1,0:T(8,128)S(1)}, u32[]{:S(2)}, u32[]{:S(2)}) collective-permute-start(f32[2,66,1]{2,1,0:T(8,128)S(1)} %get-tuple-element.704), channel_id=1, source_target_pairs={{0,1},{1,2},{2,3},{3,4},{4,5},{5,6},{6,7},{7,0},{8,9},{9,10},{10,1... | collective-permute-start | bytes 1592 | tf_op jit(solution)/shard_map/while/body/eval_jaxpr/ppermute | solution.py:42
  187.7 6.3 %collective-permute-start.4 = (f32[3,1]{1,0:T(4,128)S(1)}, f32[3,1]{1,0:T(4,128)S(1)}, u32[]{:S(2)}, u32[]{:S(2)}) collective-permute-start(f32[3,1]{1,0:T(4,128)S(1)} %slice.651), channel_id=1, source_target_pairs={{0,1},{1,2},{2,3},{3,4},{4,5},{5,6},{6,7},{7,0},{8,9},{9,10},{10,1... | collective-permute-start | bytes 44 | tf_op jit(solution)/shard_map/while/body/eval_jaxpr/ppermute | solution.py:22
  201.2 4.5 %collective-permute-start.7 = (f32[3,129]{1,0:T(4,128)S(1)}, f32[3,129]{1,0:T(4,128)S(1)}, u32[]{:S(2)}, u32[]{:S(2)}) collective-permute-start(f32[3,129]{1,0:T(4,128)S(1)} %collective-permute-done.6), channel_id=1, source_target_pairs={{0,4},{1,5},{2,6},{3,7},{4,0},{5,1},{6,2},{7,3},{8,12},{9,13},{10,... | collective-permute-start | bytes 4652 | tf_op jit(solution)/shard_map/while/body/eval_jaxpr/ppermute | solution.py:32
  209.3 4.4 %collective-permute-start.2 = (f32[2,66,1]{2,1,0:T(8,128)S(1)}, f32[2,66,1]{2,1,0:T(8,128)S(1)}, u32[]{:S(2)}, u32[]{:S(2)}) collective-permute-start(f32[2,66,1]{2,1,0:T(8,128)S(1)} %get-tuple-element.703), channel_id=1, source_target_pairs={{1,0},{2,1},{3,2},{4,3},{5,4},{6,5},{7,6},{0,7},{9,8},{10,9},{11,1... | collective-permute-start | bytes 1592 | tf_op jit(solution)/shard_map/while/body/eval_jaxpr/ppermute | solution.py:43
  209.4 7.1 %collective-permute-start.3 = (f32[2,66,1]{2,1,0:T(8,128)S(1)}, f32[2,66,1]{2,1,0:T(8,128)S(1)}, u32[]{:S(2)}, u32[]{:S(2)}) collective-permute-start(f32[2,66,1]{2,1,0:T(8,128)S(1)} %get-tuple-element.704), channel_id=1, source_target_pairs={{0,1},{1,2},{2,3},{3,4},{4,5},{5,6},{6,7},{7,0},{8,9},{9,10},{10,1... | collective-permute-start | bytes 1592 | tf_op jit(solution)/shard_map/while/body/eval_jaxpr/ppermute | solution.py:42
  217.1 6.3 %collective-permute-start.4 = (f32[3,1]{1,0:T(4,128)S(1)}, f32[3,1]{1,0:T(4,128)S(1)}, u32[]{:S(2)}, u32[]{:S(2)}) collective-permute-start(f32[3,1]{1,0:T(4,128)S(1)} %slice.651), channel_id=1, source_target_pairs={{0,1},{1,2},{2,3},{3,4},{4,5},{5,6},{6,7},{7,0},{8,9},{9,10},{10,1... | collective-permute-start | bytes 44 | tf_op jit(solution)/shard_map/while/body/eval_jaxpr/ppermute | solution.py:22
  230.6 4.5 %collective-permute-start.7 = (f32[3,129]{1,0:T(4,128)S(1)}, f32[3,129]{1,0:T(4,128)S(1)}, u32[]{:S(2)}, u32[]{:S(2)}) collective-permute-start(f32[3,129]{1,0:T(4,128)S(1)} %collective-permute-done.6), channel_id=1, source_target_pairs={{0,4},{1,5},{2,6},{3,7},{4,0},{5,1},{6,2},{7,3},{8,12},{9,13},{10,... | collective-permute-start | bytes 4652 | tf_op jit(solution)/shard_map/while/body/eval_jaxpr/ppermute | solution.py:32
  238.7 4.4 %collective-permute-start.2 = (f32[2,66,1]{2,1,0:T(8,128)S(1)}, f32[2,66,1]{2,1,0:T(8,128)S(1)}, u32[]{:S(2)}, u32[]{:S(2)}) collective-permute-start(f32[2,66,1]{2,1,0:T(8,128)S(1)} %get-tuple-element.703), channel_id=1, source_target_pairs={{1,0},{2,1},{3,2},{4,3},{5,4},{6,5},{7,6},{0,7},{9,8},{10,9},{11,1... | collective-permute-start | bytes 1592 | tf_op jit(solution)/shard_map/while/body/eval_jaxpr/ppermute | solution.py:43
  238.8 7.1 %collective-permute-start.3 = (f32[2,66,1]{2,1,0:T(8,128)S(1)}, f32[2,66,1]{2,1,0:T(8,128)S(1)}, u32[]{:S(2)}, u32[]{:S(2)}) collective-permute-start(f32[2,66,1]{2,1,0:T(8,128)S(1)} %get-tuple-element.704), channel_id=1, source_target_pairs={{0,1},{1,2},{2,3},{3,4},{4,5},{5,6},{6,7},{7,0},{8,9},{9,10},{10,1... | collective-permute-start | bytes 1592 | tf_op jit(solution)/shard_map/while/body/eval_jaxpr/ppermute | solution.py:42
  246.5 6.3 %collective-permute-start.4 = (f32[3,1]{1,0:T(4,128)S(1)}, f32[3,1]{1,0:T(4,128)S(1)}, u32[]{:S(2)}, u32[]{:S(2)}) collective-permute-start(f32[3,1]{1,0:T(4,128)S(1)} %slice.651), channel_id=1, source_target_pairs={{0,1},{1,2},{2,3},{3,4},{4,5},{5,6},{6,7},{7,0},{8,9},{9,10},{10,1... | collective-permute-start | bytes 44 | tf_op jit(solution)/shard_map/while/body/eval_jaxpr/ppermute | solution.py:22
  256.4 3.6 collective-permute-start.6
  260.0 4.5 %collective-permute-start.7 = (f32[3,129]{1,0:T(4,128)S(1)}, f32[3,129]{1,0:T(4,128)S(1)}, u32[]{:S(2)}, u32[]{:S(2)}) collective-permute-start(f32[3,129]{1,0:T(4,128)S(1)} %collective-permute-done.6), channel_id=1, source_target_pairs={{0,4},{1,5},{2,6},{3,7},{4,0},{5,1},{6,2},{7,3},{8,12},{9,13},{10,... | collective-permute-start | bytes 4652 | tf_op jit(solution)/shard_map/while/body/eval_jaxpr/ppermute | solution.py:32
  268.1 4.4 %collective-permute-start.2 = (f32[2,66,1]{2,1,0:T(8,128)S(1)}, f32[2,66,1]{2,1,0:T(8,128)S(1)}, u32[]{:S(2)}, u32[]{:S(2)}) collective-permute-start(f32[2,66,1]{2,1,0:T(8,128)S(1)} %get-tuple-element.703), channel_id=1, source_target_pairs={{1,0},{2,1},{3,2},{4,3},{5,4},{6,5},{7,6},{0,7},{9,8},{10,9},{11,1... | collective-permute-start | bytes 1592 | tf_op jit(solution)/shard_map/while/body/eval_jaxpr/ppermute | solution.py:43
  268.2 7.1 %collective-permute-start.3 = (f32[2,66,1]{2,1,0:T(8,128)S(1)}, f32[2,66,1]{2,1,0:T(8,128)S(1)}, u32[]{:S(2)}, u32[]{:S(2)}) collective-permute-start(f32[2,66,1]{2,1,0:T(8,128)S(1)} %get-tuple-element.704), channel_id=1, source_target_pairs={{0,1},{1,2},{2,3},{3,4},{4,5},{5,6},{6,7},{7,0},{8,9},{9,10},{10,1... | collective-permute-start | bytes 1592 | tf_op jit(solution)/shard_map/while/body/eval_jaxpr/ppermute | solution.py:42
  275.9 6.3 %collective-permute-start.4 = (f32[3,1]{1,0:T(4,128)S(1)}, f32[3,1]{1,0:T(4,128)S(1)}, u32[]{:S(2)}, u32[]{:S(2)}) collective-permute-start(f32[3,1]{1,0:T(4,128)S(1)} %slice.651), channel_id=1, source_target_pairs={{0,1},{1,2},{2,3},{3,4},{4,5},{5,6},{6,7},{7,0},{8,9},{9,10},{10,1... | collective-permute-start | bytes 44 | tf_op jit(solution)/shard_map/while/body/eval_jaxpr/ppermute | solution.py:22
  282.2 3.6 collective-permute-start.5
  289.4 4.5 %collective-permute-start.7 = (f32[3,129]{1,0:T(4,128)S(1)}, f32[3,129]{1,0:T(4,128)S(1)}, u32[]{:S(2)}, u32[]{:S(2)}) collective-permute-start(f32[3,129]{1,0:T(4,128)S(1)} %collective-permute-done.6), channel_id=1, source_target_pairs={{0,4},{1,5},{2,6},{3,7},{4,0},{5,1},{6,2},{7,3},{8,12},{9,13},{10,... | collective-permute-start | bytes 4652 | tf_op jit(solution)/shard_map/while/body/eval_jaxpr/ppermute | solution.py:32
  297.5 4.4 %collective-permute-start.2 = (f32[2,66,1]{2,1,0:T(8,128)S(1)}, f32[2,66,1]{2,1,0:T(8,128)S(1)}, u32[]{:S(2)}, u32[]{:S(2)}) collective-permute-start(f32[2,66,1]{2,1,0:T(8,128)S(1)} %get-tuple-element.703), channel_id=1, source_target_pairs={{1,0},{2,1},{3,2},{4,3},{5,4},{6,5},{7,6},{0,7},{9,8},{10,9},{11,1... | collective-permute-start | bytes 1592 | tf_op jit(solution)/shard_map/while/body/eval_jaxpr/ppermute | solution.py:43
  297.6 7.1 %collective-permute-start.3 = (f32[2,66,1]{2,1,0:T(8,128)S(1)}, f32[2,66,1]{2,1,0:T(8,128)S(1)}, u32[]{:S(2)}, u32[]{:S(2)}) collective-permute-start(f32[2,66,1]{2,1,0:T(8,128)S(1)} %get-tuple-element.704), channel_id=1, source_target_pairs={{0,1},{1,2},{2,3},{3,4},{4,5},{5,6},{6,7},{7,0},{8,9},{9,10},{10,1... | collective-permute-start | bytes 1592 | tf_op jit(solution)/shard_map/while/body/eval_jaxpr/ppermute | solution.py:42
  305.3 6.3 %collective-permute-start.4 = (f32[3,1]{1,0:T(4,128)S(1)}, f32[3,1]{1,0:T(4,128)S(1)}, u32[]{:S(2)}, u32[]{:S(2)}) collective-permute-start(f32[3,1]{1,0:T(4,128)S(1)} %slice.651), channel_id=1, source_target_pairs={{0,1},{1,2},{2,3},{3,4},{4,5},{5,6},{6,7},{7,0},{8,9},{9,10},{10,1... | collective-permute-start | bytes 44 | tf_op jit(solution)/shard_map/while/body/eval_jaxpr/ppermute | solution.py:22
  318.8 4.5 %collective-permute-start.7 = (f32[3,129]{1,0:T(4,128)S(1)}, f32[3,129]{1,0:T(4,128)S(1)}, u32[]{:S(2)}, u32[]{:S(2)}) collective-permute-start(f32[3,129]{1,0:T(4,128)S(1)} %collective-permute-done.6), channel_id=1, source_target_pairs={{0,4},{1,5},{2,6},{3,7},{4,0},{5,1},{6,2},{7,3},{8,12},{9,13},{10,... | collective-permute-start | bytes 4652 | tf_op jit(solution)/shard_map/while/body/eval_jaxpr/ppermute | solution.py:32
  326.9 4.4 %collective-permute-start.2 = (f32[2,66,1]{2,1,0:T(8,128)S(1)}, f32[2,66,1]{2,1,0:T(8,128)S(1)}, u32[]{:S(2)}, u32[]{:S(2)}) collective-permute-start(f32[2,66,1]{2,1,0:T(8,128)S(1)} %get-tuple-element.703), channel_id=1, source_target_pairs={{1,0},{2,1},{3,2},{4,3},{5,4},{6,5},{7,6},{0,7},{9,8},{10,9},{11,1... | collective-permute-start | bytes 1592 | tf_op jit(solution)/shard_map/while/body/eval_jaxpr/ppermute | solution.py:43
  327.0 7.1 %collective-permute-start.3 = (f32[2,66,1]{2,1,0:T(8,128)S(1)}, f32[2,66,1]{2,1,0:T(8,128)S(1)}, u32[]{:S(2)}, u32[]{:S(2)}) collective-permute-start(f32[2,66,1]{2,1,0:T(8,128)S(1)} %get-tuple-element.704), channel_id=1, source_target_pairs={{0,1},{1,2},{2,3},{3,4},{4,5},{5,6},{6,7},{7,0},{8,9},{9,10},{10,1... | collective-permute-start | bytes 1592 | tf_op jit(solution)/shard_map/while/body/eval_jaxpr/ppermute | solution.py:42
  334.7 6.3 %collective-permute-start.4 = (f32[3,1]{1,0:T(4,128)S(1)}, f32[3,1]{1,0:T(4,128)S(1)}, u32[]{:S(2)}, u32[]{:S(2)}) collective-permute-start(f32[3,1]{1,0:T(4,128)S(1)} %slice.651), channel_id=1, source_target_pairs={{0,1},{1,2},{2,3},{3,4},{4,5},{5,6},{6,7},{7,0},{8,9},{9,10},{10,1... | collective-permute-start | bytes 44 | tf_op jit(solution)/shard_map/while/body/eval_jaxpr/ppermute | solution.py:22
  344.6 3.6 collective-permute-start.6
  348.2 4.5 %collective-permute-start.7 = (f32[3,129]{1,0:T(4,128)S(1)}, f32[3,129]{1,0:T(4,128)S(1)}, u32[]{:S(2)}, u32[]{:S(2)}) collective-permute-start(f32[3,129]{1,0:T(4,128)S(1)} %collective-permute-done.6), channel_id=1, source_target_pairs={{0,4},{1,5},{2,6},{3,7},{4,0},{5,1},{6,2},{7,3},{8,12},{9,13},{10,... | collective-permute-start | bytes 4652 | tf_op jit(solution)/shard_map/while/body/eval_jaxpr/ppermute | solution.py:32
  356.4 4.4 %collective-permute-start.2 = (f32[2,66,1]{2,1,0:T(8,128)S(1)}, f32[2,66,1]{2,1,0:T(8,128)S(1)}, u32[]{:S(2)}, u32[]{:S(2)}) collective-permute-start(f32[2,66,1]{2,1,0:T(8,128)S(1)} %get-tuple-element.703), channel_id=1, source_target_pairs={{1,0},{2,1},{3,2},{4,3},{5,4},{6,5},{7,6},{0,7},{9,8},{10,9},{11,1... | collective-permute-start | bytes 1592 | tf_op jit(solution)/shard_map/while/body/eval_jaxpr/ppermute | solution.py:43
  356.4 7.1 %collective-permute-start.3 = (f32[2,66,1]{2,1,0:T(8,128)S(1)}, f32[2,66,1]{2,1,0:T(8,128)S(1)}, u32[]{:S(2)}, u32[]{:S(2)}) collective-permute-start(f32[2,66,1]{2,1,0:T(8,128)S(1)} %get-tuple-element.704), channel_id=1, source_target_pairs={{0,1},{1,2},{2,3},{3,4},{4,5},{5,6},{6,7},{7,0},{8,9},{9,10},{10,1... | collective-permute-start | bytes 1592 | tf_op jit(solution)/shard_map/while/body/eval_jaxpr/ppermute | solution.py:42
  364.1 6.3 %collective-permute-start.4 = (f32[3,1]{1,0:T(4,128)S(1)}, f32[3,1]{1,0:T(4,128)S(1)}, u32[]{:S(2)}, u32[]{:S(2)}) collective-permute-start(f32[3,1]{1,0:T(4,128)S(1)} %slice.651), channel_id=1, source_target_pairs={{0,1},{1,2},{2,3},{3,4},{4,5},{5,6},{6,7},{7,0},{8,9},{9,10},{10,1... | collective-permute-start | bytes 44 | tf_op jit(solution)/shard_map/while/body/eval_jaxpr/ppermute | solution.py:22
  370.4 3.6 collective-permute-start.5
  374.0 3.6 collective-permute-start.6
  377.6 4.5 %collective-permute-start.7 = (f32[3,129]{1,0:T(4,128)S(1)}, f32[3,129]{1,0:T(4,128)S(1)}, u32[]{:S(2)}, u32[]{:S(2)}) collective-permute-start(f32[3,129]{1,0:T(4,128)S(1)} %collective-permute-done.6), channel_id=1, source_target_pairs={{0,4},{1,5},{2,6},{3,7},{4,0},{5,1},{6,2},{7,3},{8,12},{9,13},{10,... | collective-permute-start | bytes 4652 | tf_op jit(solution)/shard_map/while/body/eval_jaxpr/ppermute | solution.py:32
  (46 other events, 157.5 us)
Sparse Core Ops, SparseCore 0:
  18.3 15.4 all-gather.1
where the time goes:
time: 391 us
  waiting for transfers between devices  304 us (78%)
  starting transfers between devices  43.6 us (11%)
  between operations  14.8 us (4%)
  other arithmetic  13.3 us (3%)
  local copies, waits for them, and re-layouts  13.1 us (3%)
    ppermute x36, waiting for transfers between devices, partner(): lax.ppermute(value, axis, [(i, i ^ 1 << stride) for i in range(lax.axis_s...  135 us
    ppermute x13, waiting for transfers between devices, shifted(): return lax.ppermute(value, axis, pairs)  75.5 us
    ppermute x24, waiting for transfers between devices, extended(): before = lax.ppermute(last, axis, up)  56.6 us
    ppermute x24, waiting for transfers between devices, extended(): after = lax.ppermute(first, axis, down)  36.5 us
    ppermute x24, starting transfers between devices, extended(): before = lax.ppermute(last, axis, up)  27.6 us
    ppermute x24, starting transfers between devices, extended(): after = lax.ppermute(first, axis, down)  8.49 us
  transfers between devices with their start and end apart: 99, of which 98 were waited for; matrix products, arithmetic and copies ran while one was open for 5% of the time, Pallas kernels for 0%

commit v1 on v0

v1 whole, which is shorter than its diff:
```python
import functools

import jax
import jax.numpy as jnp
from jax import lax
from jax.experimental import pallas as pl
from jax.experimental.pallas import tpu as pltpu
from jax.sharding import PartitionSpec as P

SUB = 12
PAD = 8
LANES = 16
FIELDS = 13

strength_scale = 4.0
hibler_decay = 20.0
mass_rate = 16.0
water_drag = 1.0
coriolis = 0.5


def halo_rows():
    return -(-SUB // 8) * 8


def expand_into(mask_ref, blocks_ref):
    block_rows, block_cols = blocks_ref.shape
    height, breadth = mask_ref.shape
    tall, wide = height // block_rows, breadth // block_cols
    counted = blocks_ref[...].astype(jnp.float32)
    lane = lax.broadcasted_iota(jnp.int32, (block_rows, breadth), 1)
    spread = jnp.zeros((block_rows, breadth), jnp.float32)
    for b in range(block_cols):
        inside = (lane >= b * wide) & (lane < (b + 1) * wide)
        spread = jnp.where(inside, counted[:, b : b + 1], spread)
    for b in range(block_rows):
        mask_ref[b * tall : (b + 1) * tall, :] = jnp.broadcast_to(
            spread[b : b + 1, :], (tall, breadth)
        )


def kernel(
    nr,
    nc,
    vel_ref,
    str_ref,
    wind_ref,
    cur_ref,
    area_ref,
    vol_ref,
    iw_ref,
    ih_ref,
    land_ref,
    ice_ref,
    vel_out,
    str_out,
    strips,
    main,
    side,
    pack_e,
    pack_w,
    land_e,
    land_w,
    ocean_ref,
    icy_ref,
    send_sem,
    recv_sem,
    x_send,
    x_recv,
    f_send,
    f_recv,
    own_sem,
):
    hr = halo_rows()
    height, breadth = iw_ref.shape
    cats = area_ref.shape[0]
    rows = height + 2 * hr
    per = breadth // LANES
    groups = pack_e.shape[0]
    r = lax.axis_index("row")
    c = lax.axis_index("col")
    east = lax.rem(c + 1, nc)
    west = lax.rem(c + nc - 1, nc)
    mirror = nc - 1 - c
    m_e = lax.rem(mirror + nc - 1, nc)
    m_w = lax.rem(mirror + 1, nc)
    partner = r + 1 - 2 * lax.rem(r, 2)
    is_top = r == nr - 1
    not_top = r < nr - 1
    above_bottom = r > 0
    self_e = jnp.logical_and(is_top, m_e == c)
    self_w = jnp.logical_and(is_top, m_w == c)
    other_e = jnp.logical_and(is_top, m_e != c)
    other_w = jnp.logical_and(is_top, m_w != c)
    others = [lax.rem(r + 2 * k, nr) for k in range(1, nr // 2)]

    barrier = pltpu.get_barrier_semaphore()

    def greet(row, col):
        pl.semaphore_signal(
            barrier,
            inc=1,
            device_id={"row": row, "col": col},
            device_id_type=pl.DeviceIdType.MESH,
        )

    greet(r, east)
    greet(r, west)
    greet(partner, c)
    for other in others:
        greet(other, c)

    @pl.when(not_top)
    def _():
        greet(r + 1, c)
        greet(r + 1, east)
        greet(r + 1, west)

    @pl.when(above_bottom)
    def _():
        greet(r - 1, c)
        greet(r - 1, east)
        greet(r - 1, west)

    @pl.when(is_top)
    def _():
        greet(r, mirror)

    @pl.when(other_e)
    def _():
        greet(r, m_e)

    @pl.when(other_w)
    def _():
        greet(r, m_w)

    own = pl.ds(pl.multiple_of(r * height, height), height)
    locals_ = [
        pltpu.make_async_copy(area_ref, strips.at[0:cats, own, :], own_sem.at[0]),
        pltpu.make_async_copy(vol_ref, strips.at[cats : 2 * cats, own, :], own_sem.at[1]),
    ]
    for copy in locals_:
        copy.start()

    expand_into(ocean_ref, land_ref)
    expand_into(icy_ref, ice_ref)
    first = PAD + hr
    lane = lax.broadcasted_iota(jnp.int32, (8, breadth), 1)
    zero = jnp.zeros((8, breadth), jnp.float32)
    for f in range(5):
        for at in (0, PAD + rows):
            main[f, at : at + 8, :] = zero
            side[f, at : at + 8, :] = zero
    for k in range(height // 8):
        here = slice(8 * k, 8 * k + 8)
        there = slice(first + 8 * k, first + 8 * k + 8)
        area = area_ref[0, here, :]
        volume = vol_ref[0, here, :]
        for n in range(1, cats):
            area = area + area_ref[n, here, :]
            volume = volume + vol_ref[n, here, :]
        ocean = ocean_ref[here, :]
        icy = icy_ref[here, :]
        strength = strength_scale * volume * jnp.exp(-hibler_decay * (1.0 - area)) * ocean
        inertia = mass_rate * (1.0 + volume)
        turning = coriolis * (1.0 + volume)
        damped = inertia + water_drag
        live = ocean * icy / (damped * damped + turning * turning)
        ca = damped * live
        cb = turning * live
        rest = ocean * (1.0 - icy)
        cu = cur_ref[0, here, :]
        cv = cur_ref[1, here, :]
        gu = wind_ref[0, here, :] + water_drag * cu
        gv = wind_ref[1, here, :] + water_drag * cv
        values = [
            vel_ref[0, here, :],
            vel_ref[1, here, :],
            str_ref[0, here, :],
            str_ref[1, here, :],
            str_ref[2, here, :],
            ca * gu + cb * gv + rest * cu,
            ca * gv - cb * gu + rest * cv,
            ca,
            cb,
            inertia,
            strength * (1.0 / 3.0),
            0.5 * iw_ref[here, :],
            0.5 * ih_ref[here, :],
        ]
        for f, value in enumerate(values):
            main[f, there, :] = value
        for g in range(groups):
            packed_e = zero
            packed_w = zero
            for s in range(per):
                f = g * per + s
                if f >= FIELDS:
                    break
                slot = (lane >= s * LANES) & (lane < (s + 1) * LANES)
                value = values[f]
                turn_w = s * LANES
                turn_e = (s * LANES + LANES) % breadth
                packed_w = jnp.where(
                    slot, pltpu.roll(value, turn_w, 1) if turn_w else value, packed_w
                )
                packed_e = jnp.where(
                    slot, pltpu.roll(value, turn_e, 1) if turn_e else value, packed_e
                )
            pack_e[g, here, :] = packed_e
            pack_w[g, here, :] = packed_w

    peers = 3 + len(others) + 3 * not_top.astype(jnp.int32) + 3 * above_bottom.astype(jnp.int32)
    peers = peers + is_top.astype(jnp.int32)
    peers = peers + other_e.astype(jnp.int32) + other_w.astype(jnp.int32)
    pl.semaphore_wait(barrier, peers)

    def remote(src, dst, send, recv, row, col):
        return pltpu.make_async_remote_copy(
            src_ref=src,
            dst_ref=dst,
            send_sem=send,
            recv_sem=recv,
            device_id={"row": row, "col": col},
            device_id_type=pl.DeviceIdType.MESH,
        )

    mid = slice(hr, hr + height)
    low = slice(0, hr)
    high = slice(hr + height, rows)
    top_rows = slice(height - hr, height)
    bottom_rows = slice(0, hr)

    def halo(slot, src, dst, row, col):
        return remote(src, dst, send_sem.at[slot], recv_sem.at[slot], row, col)

    to_west = halo(0, pack_w, land_e.at[:, mid, :], r, west)
    to_east = halo(1, pack_e, land_w.at[:, mid, :], r, east)
    main_top = main.at[:, first + height - hr : first + height, :]
    main_bottom = main.at[:, first : first + hr, :]
    main_south = main.at[:, PAD : PAD + hr, :]
    main_north = main.at[:, first + height : first + height + hr, :]
    up = [
        halo(2, main_top, main_south, r + 1, c),
        halo(4, pack_w.at[:, top_rows, :], land_e.at[:, low, :], r + 1, west),
        halo(5, pack_e.at[:, top_rows, :], land_w.at[:, low, :], r + 1, east),
    ]
    down = [
        halo(3, main_bottom, main_north, r - 1, c),
        halo(6, pack_w.at[:, bottom_rows, :], land_e.at[:, high, :], r - 1, west),
        halo(7, pack_e.at[:, bottom_rows, :], land_w.at[:, high, :], r - 1, east),
    ]
    over = remote(main_top, main_north, send_sem.at[8], recv_sem.at[3], r, mirror)
    over_w = remote(
        pack_w.at[:, top_rows, :], land_e.at[:, high, :], send_sem.at[9], recv_sem.at[6], r, m_w
    )
    over_e = remote(
        pack_e.at[:, top_rows, :], land_w.at[:, high, :], send_sem.at[10], recv_sem.at[7], r, m_e
    )

    @pl.when(is_top)
    def _():
        over.start()

    @pl.when(other_w)
    def _():
        over_w.start()

    @pl.when(other_e)
    def _():
        over_e.start()

    @pl.when(self_w)
    def _():
        land_e[:, high, :] = pack_w[:, top_rows, :]

    @pl.when(self_e)
    def _():
        land_w[:, high, :] = pack_e[:, top_rows, :]

    to_west.start()
    to_east.start()

    @pl.when(not_top)
    def _():
        for copy in up:
            copy.start()

    @pl.when(above_bottom)
    def _():
        for copy in down:
            copy.start()

    crossing = []
    for k, other in enumerate(others):
        for part, ref in enumerate((area_ref, vol_ref)):
            crossing.append(
                remote(
                    ref,
                    strips.at[part * cats : (part + 1) * cats, own, :],
                    x_send.at[2 * k + part],
                    x_recv.at[2 * k + part],
                    other,
                    c,
                )
            )
    for copy in crossing:
        copy.start()
    forwards = []
    for part, ref in enumerate((area_ref, vol_ref)):
        forwards.append(
            remote(
                ref,
                strips.at[part * cats : (part + 1) * cats, own, :],
                f_send.at[part],
                f_recv.at[part],
                partner,
                c,
            )
        )
    for copy in forwards:
        copy.start()

    @pl.when(r == 0)
    def _():
        for f in range(FIELDS):
            main[f, PAD : PAD + hr, :] = jnp.zeros((hr, breadth), jnp.float32)
        for g in range(groups):
            land_e[g, low, :] = jnp.zeros((hr, breadth), jnp.float32)
            land_w[g, low, :] = jnp.zeros((hr, breadth), jnp.float32)

    to_west.wait()
    to_east.wait()

    @pl.when(not_top)
    def _():
        for copy in up:
            copy.wait_send()
        for copy in down:
            copy.wait_recv()

    @pl.when(above_bottom)
    def _():
        for copy in down:
            copy.wait_send()
        for copy in up:
            copy.wait_recv()

    @pl.when(is_top)
    def _():
        over.wait()

    @pl.when(other_w)
    def _():
        over_w.wait()

    @pl.when(other_e)
    def _():
        over_e.wait()

    for k in range(rows // 8):
        here = slice(8 * k, 8 * k + 8)
        there = slice(PAD + 8 * k, PAD + 8 * k + 8)
        for f in range(FIELDS):
            g, s = divmod(f, per)
            turn_e = (breadth - s * LANES) % breadth
            turn_w = (breadth - LANES - s * LANES) % breadth
            from_e = land_e[g, here, :]
            from_w = land_w[g, here, :]
            from_e = pltpu.roll(from_e, turn_e, 1) if turn_e else from_e
            from_w = pltpu.roll(from_w, turn_w, 1) if turn_w else from_w
            side[f, there, :] = jnp.where(
                lane < LANES, from_e, jnp.where(lane >= breadth - LANES, from_w, 0.0)
            )

    sub = lax.broadcasted_iota(jnp.int32, (8, breadth), 0)
    first_lane = lane == 0
    last_lane = lane == breadth - 1
    fold_here = (sub == 7) & is_top
    backwards = breadth - 1 - lane

    def west_of(a, b):
        ra = pltpu.roll(a, 1, 1)
        rb = pltpu.roll(b, 1, 1)
        return jnp.where(first_lane, rb, ra), jnp.where(first_lane, ra, rb)

    def east_of(a, b):
        ra = pltpu.roll(a, breadth - 1, 1)
        rb = pltpu.roll(b, breadth - 1, 1)
        return jnp.where(last_lane, rb, ra), jnp.where(last_lane, ra, rb)

    tiles = (main, side)
    last_own = first + height - 1
    last_north = PAD + rows - 1

    def cycle(_, carry):
        for k in range(rows // 8):
            here = slice(PAD + 8 * k, PAD + 8 * k + 8)
            south = slice(PAD + 8 * k - 1, PAD + 8 * k + 7)
            us, ud, vs, vd = [], [], [], []
            for t in tiles:
                u, v = t[0, here, :], t[1, here, :]
                su, sv = t[0, south, :], t[1, south, :]
                us.append(u + su)
                ud.append(u - su)
                vs.append(v + sv)
                vd.append(v - sv)
            wus, wud, wvs, wvd = west_of(*us), west_of(*ud), west_of(*vs), west_of(*vd)
            for i, t in enumerate(tiles):
                hw, hh = t[11, here, :], t[12, here, :]
                gux = hw * (us[i] - wus[i])
                gvx = hw * (vs[i] - wvs[i])
                guy = hh * (ud[i] + wud[i])
                gvy = hh * (vd[i] + wvd[i])
                div = gux + gvy
                ten = gux - gvy
                shear = guy + gvx
                deform = jnp.sqrt(div * div + 0.25 * (ten * ten + shear * shear))
                w = t[10, here, :] / (deform + 0.5)
                t[2, here, :] = t[2, here, :] * (2.0 / 3.0) + w * (div - deform)
                t[3, here, :] = t[3, here, :] * (2.0 / 3.0) + (0.25 * w) * ten
                t[4, here, :] = t[4, here, :] * (2.0 / 3.0) + (0.125 * w) * shear

        def edge(row):
            lines = [t[f, row : row + 1, :] for t in tiles for f in (2, 3, 4)]
            stacked = jnp.concatenate(lines + [lines[0], lines[0]], axis=0)
            return jnp.take_along_axis(stacked, backwards, axis=1)

        own_edge = edge(last_own)
        north_edge = edge(last_north)
        for i, t in enumerate(tiles):
            for f in range(3):
                line = 3 * i + f
                t[2 + f, last_north + 1 : last_north + 2, :] = own_edge[line : line + 1, :]

        for k in range(rows // 8):
            here = slice(PAD + 8 * k, PAD + 8 * k + 8)
            north = slice(PAD + 8 * k + 1, PAD + 8 * k + 9)
            p, d, q, e = [], [], [], []
            for i, t in enumerate(tiles):
                s1, s2, s12 = t[2, here, :], t[3, here, :], t[4, here, :]
                n1, n2, n12 = t[2, north, :], t[3, north, :], t[4, north, :]
                if PAD + 8 * k + 7 == last_own:
                    ghost = [
                        jnp.broadcast_to(
                            north_edge[3 * i + f : 3 * i + f + 1, :], (8, breadth)
                        )
                        for f in range(3)
                    ]
                    n1 = jnp.where(fold_here, ghost[0], n1)
                    n2 = jnp.where(fold_here, ghost[1], n2)
                    n12 = jnp.where(fold_here, ghost[2], n12)
                p.append((s1 + s2) + (n1 + n2))
                d.append(n12 - s12)
                q.append(s12 + n12)
                e.append((n1 - n2) - (s1 - s2))
            ep, ed, eq, ee = east_of(*p), east_of(*d), east_of(*q), east_of(*e)
            for i, t in enumerate(tiles):
                hw, hh = t[11, here, :], t[12, here, :]
                fx = hw * (0.5 * (ep[i] - p[i])) + hh * (d[i] + ed[i])
                fy = hw * (eq[i] - q[i]) + hh * (0.5 * (e[i] + ee[i]))
                inertia = t[9, here, :]
                rx = inertia * t[0, here, :] + fx
                ry = inertia * t[1, here, :] + fy
                ca, cb = t[7, here, :], t[8, here, :]
                t[0, here, :] = ca * rx + cb * ry + t[5, here, :]
                t[1, here, :] = ca * ry - cb * rx + t[6, here, :]
        return carry

    early = SUB * 3 // 4
    lax.fori_loop(0, early, cycle, 0)

    relays = []
    for k in range(len(others)):
        source = lax.rem(r + nr - 2 * (k + 1), nr)
        lines = pl.ds(pl.multiple_of(source * height, height), height)
        for part in range(2):
            crossing[2 * k + part].wait_recv()
            block = strips.at[part * cats : (part + 1) * cats, lines, :]
            slot = 2 + 2 * k + part
            copy = remote(block, block, f_send.at[slot], f_recv.at[slot], partner, c)
            copy.start()
            relays.append(copy)

    lax.fori_loop(0, SUB - early, cycle, 0)

    inner = slice(first, first + height)
    for f in range(2):
        vel_out[f] = main[f, inner, :]
    for f in range(3):
        str_out[f] = main[2 + f, inner, :]

    for copy in locals_:
        copy.wait()
    for copy in crossing:
        copy.wait_send()
    for copy in forwards + relays:
        copy.wait()


def shards(nr, nc, *operands):
    (vel, stress, wind, current, area, volume, iw, ih, land, ice, writer) = operands
    hr = halo_rows()
    height, breadth = iw.shape
    cats = area.shape[0]
    rows = height + 2 * hr
    groups = -(-FIELDS // (breadth // LANES))
    space = pl.BlockSpec(memory_space=pltpu.VMEM)
    relayed = max(2 * (nr // 2 - 1), 1)
    f32 = jnp.float32
    sent = 4 * (2 * FIELDS * hr * breadth + 2 * groups * rows * breadth + 3 * area.size)
    velocity, stresses, strips = pl.pallas_call(
        functools.partial(kernel, nr, nc),
        out_shape=(
            jax.ShapeDtypeStruct(vel.shape, f32),
            jax.ShapeDtypeStruct(stress.shape, f32),
            jax.ShapeDtypeStruct((2 * cats, nr * height, breadth), f32),
        ),
        in_specs=[space] * 10,
        out_specs=(space, space, space),
        scratch_shapes=[
            pltpu.VMEM((FIELDS, rows + 2 * PAD, breadth), f32),
            pltpu.VMEM((FIELDS, rows + 2 * PAD, breadth), f32),
            pltpu.VMEM((groups, height, breadth), f32),
            pltpu.VMEM((groups, height, breadth), f32),
            pltpu.VMEM((groups, rows, breadth), f32),
            pltpu.VMEM((groups, rows, breadth), f32),
            pltpu.VMEM((height, breadth), f32),
            pltpu.VMEM((height, breadth), f32),
            pltpu.SemaphoreType.DMA((11,)),
            pltpu.SemaphoreType.DMA((8,)),
            pltpu.SemaphoreType.DMA((relayed,)),
            pltpu.SemaphoreType.DMA((relayed,)),
            pltpu.SemaphoreType.DMA((2 + relayed,)),
            pltpu.SemaphoreType.DMA((2 + relayed,)),
            pltpu.SemaphoreType.DMA((2,)),
        ],
        compiler_params=pltpu.CompilerParams(
            collective_id=0, has_side_effects=True, vmem_limit_bytes=32 * 1024 * 1024
        ),
        cost_estimate=pl.CostEstimate(
            flops=SUB * rows * breadth * 200, bytes_accessed=sent, transcendentals=0
        ),
    )(vel, stress, wind, current, area, volume, iw, ih, land, ice)
    index = jnp.arange(writer.shape[0], dtype=jnp.int32)
    chosen = jnp.sum(jnp.where(index == lax.axis_index("col"), writer, 0))
    restart = jnp.where(chosen == lax.axis_index("row"), strips, 0.0)[None]
    return velocity, stresses, restart


def solution(mesh):
    field = P(None, "row", "col")
    flat = P("row", "col")
    return jax.shard_map(
        functools.partial(shards, mesh.shape["row"], mesh.shape["col"]),
        mesh=mesh,
        in_specs=(field,) * 6 + (flat,) * 4 + (P(),),
        out_specs=(field, field, P("row", None, None, "col")),
        check_vma=False,
    )
```

time: 391 us -> 32.4 us (0.08)
  waiting for transfers between devices: 304 us -> 0 us
  starting transfers between devices: 43.6 us -> 0 us
  Pallas kernels: 0 us -> 18.5 us
  between operations: 14.8 us -> 1.31 us
  other arithmetic: 13.3 us -> 2.45 us
    ppermute x98 -> x0, waiting for transfers between devices: 304 us -> none  [the longest x36 135 us: partner(): lax.ppermute(value, axis, [(i, i ^ 1 << stride) for i in range(lax.axis_s...]
    ppermute x98 -> x0, starting transfers between devices: 43.6 us -> none  [the longest x24 27.6 us: extended(): before = lax.ppermute(last, axis, up)]
    pallas_call x0 -> x1, Pallas kernels: none -> 18.5 us  [shards(): pl.pallas_call(functools.partial(kernel, nr, nc), out_shape=(jax.ShapeDty...]
    unnamed x27 -> x20, local copies, waits for them, and re-layouts: 1.49 us -> 9.54 us
    div x48 -> x0, other arithmetic: 5.26 us -> none  [the longest x12 2.42 us: stress_update(): (stresses[0] + relax_rate * viscous * (divergence - deform)) / (1.0 + rel...]
  transfers between devices with their start and end apart: 99 -> 0, of which waited for: 98 -> 0; matrix products, arithmetic and copies ran while one was open for 5% -> 0% of each run, Pallas kernels for 0% -> 0%
where the time goes in v1:
time: 32.4 us; the launch traced here: 31.8 us
  Pallas kernels  18.5 us (57%)
  local copies, waits for them, and re-layouts  9.54 us (29%)
  other arithmetic  2.45 us (8%)
  between operations  1.31 us (4%)
    pallas_call x1, Pallas kernels, shards(): pl.pallas_call(functools.partial(kernel, nr, nc), out_shape=(jax.ShapeDty...  18.5 us
    unnamed x20, local copies, waits for them, and re-layouts  9.54 us
    reduce_sum x1, other arithmetic, shards(): chosen = jnp.sum(jnp.where(index == lax.axis_index('col'), writer, 0))  1.29 us
    broadcast_in_dim x1, other arithmetic, shards(): restart = jnp.where(chosen == lax.axis_index('row'), strips, 0.0)[None]  1.16 us

profile of v1, /device:TPU:0, one launch (start us, length us, event | category | flops | bytes accessed | tf_op | source)
XLA Modules:
  0.0 31.8 jit_solution(13358869620070008691)
XLA Ops:
  0.6 1.3 %fusion = s32[]{:T(128)} fusion(s32[8]{0:T(128)} %param.21, s32[]{:T(128)S(6)} %axis_index.22), kind=kLoop, calls=%fused_computation.2 | loop fusion | flops 23 | bytes 40 | tf_op jit(solution)/shard_map/reduce_sum | solution.py:546
  2.6 0.8 %copy.14.land_ref = s32[16,4]{1,0:T(8,128)S(1)} copy(s32[16,4]{0,1:T(4,128)} %param.19) | data formatting | bytes 512 | tf_op args[8]
  3.3 0.8 %copy.15.ice_ref = s32[16,4]{1,0:T(8,128)S(1)} copy(s32[16,4]{0,1:T(4,128)} %param.20) | data formatting | bytes 512 | tf_op args[9]
  4.1 0.0 copy-start
  4.1 0.9 %copy-done = f32[5,64,128]{2,1,0:T(8,128)S(1)} copy-done((f32[5,64,128]{2,1,0:T(8,128)S(1)}, f32[5,64,128]{2,1,0:T(8,128)}, u32[]{:S(2)}) %copy-start) | copy-done | bytes 163864
  5.0 0.0 copy-start.1
  5.0 0.9 %copy-done.1 = f32[5,64,128]{2,1,0:T(8,128)S(1)} copy-done((f32[5,64,128]{2,1,0:T(8,128)S(1)}, f32[5,64,128]{2,1,0:T(8,128)}, u32[]{:S(2)}) %copy-start.1) | copy-done | bytes 163864
  5.9 0.0 copy-start.2
  5.9 0.9 %copy-done.2 = f32[3,64,128]{2,1,0:T(8,128)S(1)} copy-done((f32[3,64,128]{2,1,0:T(8,128)S(1)}, f32[3,64,128]{2,1,0:T(8,128)}, u32[]{:S(2)}) %copy-start.2) | copy-done | bytes 98328
  6.8 0.0 copy-start.3
  6.8 0.8 %copy-done.3 = f32[2,64,128]{2,1,0:T(8,128)S(1)} copy-done((f32[2,64,128]{2,1,0:T(8,128)S(1)}, f32[2,64,128]{2,1,0:T(8,128)}, u32[]{:S(2)}) %copy-start.3) | copy-done | bytes 65560
  7.7 0.0 copy-start.4
  7.7 0.8 %copy-done.4 = f32[2,64,128]{2,1,0:T(8,128)S(1)} copy-done((f32[2,64,128]{2,1,0:T(8,128)S(1)}, f32[2,64,128]{2,1,0:T(8,128)}, u32[]{:S(2)}) %copy-start.4) | copy-done | bytes 65560
  8.5 0.0 copy-start.5
  8.5 0.8 %copy-done.5 = f32[2,64,128]{2,1,0:T(8,128)S(1)} copy-done((f32[2,64,128]{2,1,0:T(8,128)S(1)}, f32[2,64,128]{2,1,0:T(8,128)}, u32[]{:S(2)}) %copy-start.5) | copy-done | bytes 65560
  9.3 0.0 copy-start.6
  9.3 0.8 %copy-done.6 = f32[64,128]{1,0:T(8,128)S(1)} copy-done((f32[64,128]{1,0:T(8,128)S(1)}, f32[64,128]{1,0:T(8,128)}, u32[]{:S(2)}) %copy-start.6) | copy-done | bytes 32792
  10.1 0.0 copy-start.7
  10.1 0.8 %copy-done.7 = f32[64,128]{1,0:T(8,128)S(1)} copy-done((f32[64,128]{1,0:T(8,128)S(1)}, f32[64,128]{1,0:T(8,128)}, u32[]{:S(2)}) %copy-start.7) | copy-done | bytes 32792
  10.9 18.5 %shard_map.130 = (f32[2,64,128]{2,1,0:T(8,128)S(1)}, f32[3,64,128]{2,1,0:T(8,128)S(1)}, f32[10,256,128]{2,1,0:T(8,128)S(1)}) custom-call(f32[2,64,128]{2,1,0:T(8,128)S(1)} %copy-done.3, f32[3,64,128]{2,1,0:T(8,128)S(1)} %copy-done.2, f32[2,64,128]{2,1,0:T(8,128)S(1)} %copy-done.4, f32[2,64,128]{2,1,0:T(8,128)S(1)} %copy-done.5, f32[5,64,128]{2,1,0:T(8,128)S(1)} %copy-done, ...), custom_call_target="tpu_custom_call" | custom-call | flops 29491200 | bytes 901120 | tf_op jit(solution)/shard_map/pallas_call | solution.py:512
  29.4 1.2 %select_bitcast_fusion = f32[1,10,256,128]{3,2,1,0:T(8,128)} fusion(f32[10,256,128]{2,1,0:T(8,128)S(1)} %get-tuple-element.8, pred[]{:T(512)S(6)} %eq.11), kind=kLoop, calls=%fused_computation | loop fusion | flops 327680 | bytes 2621441 | tf_op jit(solution)/shard_map/broadcast_in_dim | solution.py:547
  30.6 0.6 %copy.18 = f32[2,64,128]{2,1,0:T(8,128)} copy(f32[2,64,128]{2,1,0:T(8,128)S(1)} %get-tuple-element.12) | data formatting | bytes 131072
  31.2 0.6 %copy.19 = f32[3,64,128]{2,1,0:T(8,128)} copy(f32[3,64,128]{2,1,0:T(8,128)S(1)} %get-tuple-element.13) | data formatting | bytes 196608
Async XLA Ops:
  4.1 0.9 %copy-start = (f32[5,64,128]{2,1,0:T(8,128)S(1)}, f32[5,64,128]{2,1,0:T(8,128)}, u32[]{:S(2)}) copy-start(f32[5,64,128]{2,1,0:T(8,128)} %area_ref.1) | copy-start | bytes 491524
  5.0 0.9 %copy-start.1 = (f32[5,64,128]{2,1,0:T(8,128)S(1)}, f32[5,64,128]{2,1,0:T(8,128)}, u32[]{:S(2)}) copy-start(f32[5,64,128]{2,1,0:T(8,128)} %vol_ref.1) | copy-start | bytes 491524
  5.9 0.9 %copy-start.2 = (f32[3,64,128]{2,1,0:T(8,128)S(1)}, f32[3,64,128]{2,1,0:T(8,128)}, u32[]{:S(2)}) copy-start(f32[3,64,128]{2,1,0:T(8,128)} %str_ref.1) | copy-start | bytes 294916
  6.8 0.8 %copy-start.3 = (f32[2,64,128]{2,1,0:T(8,128)S(1)}, f32[2,64,128]{2,1,0:T(8,128)}, u32[]{:S(2)}) copy-start(f32[2,64,128]{2,1,0:T(8,128)} %vel_ref.1) | copy-start | bytes 196612
  7.7 0.8 %copy-start.4 = (f32[2,64,128]{2,1,0:T(8,128)S(1)}, f32[2,64,128]{2,1,0:T(8,128)}, u32[]{:S(2)}) copy-start(f32[2,64,128]{2,1,0:T(8,128)} %wind_ref.1) | copy-start | bytes 196612
  8.5 0.8 %copy-start.5 = (f32[2,64,128]{2,1,0:T(8,128)S(1)}, f32[2,64,128]{2,1,0:T(8,128)}, u32[]{:S(2)}) copy-start(f32[2,64,128]{2,1,0:T(8,128)} %cur_ref.1) | copy-start | bytes 196612
  9.3 0.8 %copy-start.6 = (f32[64,128]{1,0:T(8,128)S(1)}, f32[64,128]{1,0:T(8,128)}, u32[]{:S(2)}) copy-start(f32[64,128]{1,0:T(8,128)} %iw_ref.1) | copy-start | bytes 98308
  10.1 0.8 %copy-start.7 = (f32[64,128]{1,0:T(8,128)S(1)}, f32[64,128]{1,0:T(8,128)}, u32[]{:S(2)}) copy-start(f32[64,128]{1,0:T(8,128)} %ih_ref.1) | copy-start | bytes 98308

commit v2 on v1

--- a/solution.py
+++ b/solution.py
@@ -24,37 +24,45 @@
 
 
 def expand_into(mask_ref, blocks_ref):
-    block_rows, block_cols = blocks_ref.shape
+    block_cols, block_rows = blocks_ref.shape
     height, breadth = mask_ref.shape
     tall, wide = height // block_rows, breadth // block_cols
     counted = blocks_ref[...].astype(jnp.float32)
-    lane = lax.broadcasted_iota(jnp.int32, (block_rows, breadth), 1)
-    spread = jnp.zeros((block_rows, breadth), jnp.float32)
-    for b in range(block_cols):
-        inside = (lane >= b * wide) & (lane < (b + 1) * wide)
-        spread = jnp.where(inside, counted[:, b : b + 1], spread)
+    start = wide * lax.broadcasted_iota(jnp.int32, (block_cols, breadth), 0)
+    lane = lax.broadcasted_iota(jnp.int32, (block_cols, breadth), 1)
+    inside = (lane >= start) & (lane < start + wide)
     for b in range(block_rows):
-        mask_ref[b * tall : (b + 1) * tall, :] = jnp.broadcast_to(
-            spread[b : b + 1, :], (tall, breadth)
-        )
+        spread = jnp.where(inside, counted[:, b : b + 1], 0.0)
+        line = jnp.sum(spread, axis=0, keepdims=True)
+        mask_ref[b * tall : (b + 1) * tall, :] = jnp.broadcast_to(line, (tall, breadth))
 
 
 def kernel(
     nr,
     nc,
+    vel_in,
+    str_in,
+    wind_in,
+    cur_in,
+    area_in,
+    vol_in,
+    iw_in,
+    ih_in,
+    land_in,
+    ice_in,
+    writer_in,
+    vel_out,
+    str_out,
+    strips,
+    writer_out,
     vel_ref,
     str_ref,
     wind_ref,
     cur_ref,
-    area_ref,
-    vol_ref,
     iw_ref,
     ih_ref,
     land_ref,
     ice_ref,
-    vel_out,
-    str_out,
-    strips,
     main,
     side,
     pack_e,
@@ -69,11 +77,11 @@
     x_recv,
     f_send,
     f_recv,
-    own_sem,
+    in_sem,
 ):
     hr = halo_rows()
     height, breadth = iw_ref.shape
-    cats = area_ref.shape[0]
+    cats = area_in.shape[0]
     rows = height + 2 * hr
     per = breadth // LANES
     groups = pack_e.shape[0]
@@ -94,6 +102,28 @@
     other_w = jnp.logical_and(is_top, m_w != c)
     others = [lax.rem(r + 2 * k, nr) for k in range(1, nr // 2)]
 
+    own = pl.ds(pl.multiple_of(r * height, height), height)
+    area_own = strips.at[0:cats, own, :]
+    vol_own = strips.at[cats : 2 * cats, own, :]
+    inputs = (
+        (area_in, area_own),
+        (vol_in, vol_own),
+        (land_in, land_ref),
+        (ice_in, ice_ref),
+        (vel_in, vel_ref),
+        (str_in, str_ref),
+        (wind_in, wind_ref),
+        (cur_in, cur_ref),
+        (iw_in, iw_ref),
+        (ih_in, ih_ref),
+        (writer_in, writer_out),
+    )
+    arriving = [
+        pltpu.make_async_copy(src, dst, in_sem.at[n]) for n, (src, dst) in enumerate(inputs)
+    ]
+    for copy in arriving:
+        copy.start()
+
     barrier = pltpu.get_barrier_semaphore()
 
     def greet(row, col):
@@ -134,16 +164,6 @@
     def _():
         greet(r, m_w)
 
-    own = pl.ds(pl.multiple_of(r * height, height), height)
-    locals_ = [
-        pltpu.make_async_copy(area_ref, strips.at[0:cats, own, :], own_sem.at[0]),
-        pltpu.make_async_copy(vol_ref, strips.at[cats : 2 * cats, own, :], own_sem.at[1]),
-    ]
-    for copy in locals_:
-        copy.start()
-
-    expand_into(ocean_ref, land_ref)
-    expand_into(icy_ref, ice_ref)
     first = PAD + hr
     lane = lax.broadcasted_iota(jnp.int32, (8, breadth), 1)
     zero = jnp.zeros((8, breadth), jnp.float32)
@@ -151,14 +171,19 @@
         for at in (0, PAD + rows):
             main[f, at : at + 8, :] = zero
             side[f, at : at + 8, :] = zero
+    for copy in arriving:
+        copy.wait()
+    expand_into(ocean_ref, land_ref)
+    expand_into(icy_ref, ice_ref)
     for k in range(height // 8):
         here = slice(8 * k, 8 * k + 8)
         there = slice(first + 8 * k, first + 8 * k + 8)
-        area = area_ref[0, here, :]
-        volume = vol_ref[0, here, :]
+        lines = pl.ds(pl.multiple_of(r * height + 8 * k, 8), 8)
+        area = strips[0, lines, :]
+        volume = strips[cats, lines, :]
         for n in range(1, cats):
-            area = area + area_ref[n, here, :]
-            volume = volume + vol_ref[n, here, :]
+            area = area + strips[n, lines, :]
+            volume = volume + strips[cats + n, lines, :]
         ocean = ocean_ref[here, :]
         icy = icy_ref[here, :]
         strength = strength_scale * volume * jnp.exp(-hibler_decay * (1.0 - area)) * ocean
@@ -293,11 +318,11 @@
 
     crossing = []
     for k, other in enumerate(others):
-        for part, ref in enumerate((area_ref, vol_ref)):
+        for part, ref in enumerate((area_own, vol_own)):
             crossing.append(
                 remote(
                     ref,
-                    strips.at[part * cats : (part + 1) * cats, own, :],
+                    ref,
                     x_send.at[2 * k + part],
                     x_recv.at[2 * k + part],
                     other,
@@ -307,11 +332,11 @@
     for copy in crossing:
         copy.start()
     forwards = []
-    for part, ref in enumerate((area_ref, vol_ref)):
+    for part, ref in enumerate((area_own, vol_own)):
         forwards.append(
             remote(
                 ref,
-                strips.at[part * cats : (part + 1) * cats, own, :],
+                ref,
                 f_send.at[part],
                 f_recv.at[part],
                 partner,
@@ -490,11 +515,49 @@
     for f in range(3):
         str_out[f] = main[2 + f, inner, :]
 
-    for copy in locals_:
-        copy.wait()
     for copy in crossing:
         copy.wait_send()
     for copy in forwards + relays:
+        copy.wait()
+
+
+def place(strips, vel, stress, writer, restart_out, vel_out, str_out, blank, sem):
+    r = lax.axis_index("row")
+    c = lax.axis_index("col")
+    small = [
+        pltpu.make_async_copy(vel, vel_out, sem.at[0]),
+        pltpu.make_async_copy(stress, str_out, sem.at[1]),
+    ]
+    for copy in small:
+        copy.start()
+    index = lax.broadcasted_iota(jnp.int32, writer.shape, 1)
+    chosen = jnp.sum(jnp.where(index == c, writer[...], 0))
+    fields = strips.shape[0]
+
+    @pl.when(chosen == r)
+    def _():
+        copies = [
+            pltpu.make_async_copy(strips.at[n], restart_out.at[0, n], sem.at[2 + n])
+            for n in range(fields)
+        ]
+        for copy in copies:
+            copy.start()
+        for copy in copies:
+            copy.wait()
+
+    @pl.when(chosen != r)
+    def _():
+        blank[...] = jnp.zeros(blank.shape, blank.dtype)
+        copies = [
+            pltpu.make_async_copy(blank, restart_out.at[0, n], sem.at[2 + n])
+            for n in range(fields)
+        ]
+        for copy in copies:
+            copy.start()
+        for copy in copies:
+            copy.wait()
+
+    for copy in small:
         copy.wait()
 
 
@@ -505,20 +568,36 @@
     cats = area.shape[0]
     rows = height + 2 * hr
     groups = -(-FIELDS // (breadth // LANES))
-    space = pl.BlockSpec(memory_space=pltpu.VMEM)
+    vmem = pl.BlockSpec(memory_space=pltpu.VMEM)
+    hbm = pl.BlockSpec(memory_space=pltpu.HBM)
     relayed = max(2 * (nr // 2 - 1), 1)
     f32 = jnp.float32
+    land, ice = land.T, ice.T
+    writer = writer[None]
+    inputs = [
+        pltpu.with_memory_space_constraint(x, pltpu.HBM)
+        for x in (vel, stress, wind, current, area, volume, iw, ih, land, ice, writer)
+    ]
     sent = 4 * (2 * FIELDS * hr * breadth + 2 * groups * rows * breadth + 3 * area.size)
-    velocity, stresses, strips = pl.pallas_call(
+    velocity, stresses, strips, writer = pl.pallas_call(
         functools.partial(kernel, nr, nc),
         out_shape=(
             jax.ShapeDtypeStruct(vel.shape, f32),
             jax.ShapeDtypeStruct(stress.shape, f32),
             jax.ShapeDtypeStruct((2 * cats, nr * height, breadth), f32),
+            jax.ShapeDtypeStruct(writer.shape, writer.dtype),
         ),
-        in_specs=[space] * 10,
-        out_specs=(space, space, space),
+        in_specs=[hbm] * 11,
+        out_specs=(vmem,) * 4,
         scratch_shapes=[
+            pltpu.VMEM(vel.shape, f32),
+            pltpu.VMEM(stress.shape, f32),
+            pltpu.VMEM(wind.shape, f32),
+            pltpu.VMEM(current.shape, f32),
+            pltpu.VMEM(iw.shape, f32),
+            pltpu.VMEM(ih.shape, f32),
+            pltpu.VMEM(land.shape, land.dtype),
+            pltpu.VMEM(ice.shape, ice.dtype),
             pltpu.VMEM((FIELDS, rows + 2 * PAD, breadth), f32),
             pltpu.VMEM((FIELDS, rows + 2 * PAD, breadth), f32),
             pltpu.VMEM((groups, height, breadth), f32),
@@ -533,7 +612,7 @@
             pltpu.SemaphoreType.DMA((relayed,)),
             pltpu.SemaphoreType.DMA((2 + relayed,)),
             pltpu.SemaphoreType.DMA((2 + relayed,)),
-            pltpu.SemaphoreType.DMA((2,)),
+            pltpu.SemaphoreType.DMA((11,)),
         ],
         compiler_params=pltpu.CompilerParams(
             collective_id=0, has_side_effects=True, vmem_limit_bytes=32 * 1024 * 1024
@@ -541,10 +620,22 @@
         cost_estimate=pl.CostEstimate(
             flops=SUB * rows * breadth * 200, bytes_accessed=sent, transcendentals=0
         ),
-    )(vel, stress, wind, current, area, volume, iw, ih, land, ice)
-    index = jnp.arange(writer.shape[0], dtype=jnp.int32)
-    chosen = jnp.sum(jnp.where(index == lax.axis_index("col"), writer, 0))
-    restart = jnp.where(chosen == lax.axis_index("row"), strips, 0.0)[None]
+    )(*inputs)
+    restart, velocity, stresses = pl.pallas_call(
+        place,
+        out_shape=(
+            jax.ShapeDtypeStruct((1,) + strips.shape, f32),
+            jax.ShapeDtypeStruct(vel.shape, f32),
+            jax.ShapeDtypeStruct(stress.shape, f32),
+        ),
+        in_specs=[vmem] * 4,
+        out_specs=(hbm,) * 3,
+        scratch_shapes=[
+            pltpu.VMEM(strips.shape[1:], f32),
+            pltpu.SemaphoreType.DMA((2 + 2 * cats,)),
+        ],
+        compiler_params=pltpu.CompilerParams(vmem_limit_bytes=4 * 1024 * 1024),
+    )(strips, velocity, stresses, writer)
     return velocity, stresses, restart
 
 

time: 32.4 us -> 20.8 us (0.64); the launches traced: 31.8 us -> 20.7 us
  local copies, waits for them, and re-layouts: 9.54 us -> 0 us
  other arithmetic: 2.45 us -> 0 us
  Pallas kernels: 18.5 us -> 20 us
  between operations: 1.31 us -> 0.64 us
    unnamed x20 -> x0, local copies, waits for them, and re-layouts: 9.54 us -> none
    pallas_call x0 -> x1, Pallas kernels: none -> 1.31 us  [shards(): pl.pallas_call(place, out_shape=(jax.ShapeDtypeStruct((1,) + strips.shape...]
    reduce_sum x1 -> x0, other arithmetic: 1.29 us -> none  [shards(): chosen = jnp.sum(jnp.where(index == lax.axis_index('col'), writer, 0))]
    broadcast_in_dim x1 -> x0, other arithmetic: 1.16 us -> none  [shards(): restart = jnp.where(chosen == lax.axis_index('row'), strips, 0.0)[None]]
where the time goes in v2:
time: 20.8 us; the launch traced here: 20.7 us
  Pallas kernels  20 us (96%)
  between operations  0.64 us (3%)
    pallas_call x1, Pallas kernels, shards(): pl.pallas_call(functools.partial(kernel, nr, nc), out_shape=(jax.ShapeDty...  18.7 us
    pallas_call x1, Pallas kernels, shards(): pl.pallas_call(place, out_shape=(jax.ShapeDtypeStruct((1,) + strips.shape...  1.31 us

profile of v2, /device:TPU:0, one launch (start us, length us, event | category | flops | bytes accessed | tf_op | source)
XLA Modules:
  0.0 20.7 jit_solution(6183079642911458030)
XLA Ops:
  0.6 18.7 %shard_map.130 = (f32[2,64,128]{2,1,0:T(8,128)S(1)}, f32[3,64,128]{2,1,0:T(8,128)S(1)}, f32[10,256,128]{2,1,0:T(8,128)S(1)}, s32[1,8]{1,0:T(1,128)S(1)}) custom-call(f32[2,64,128]{2,1,0:T(8,128)} %vel_in.1, f32[3,64,128]{2,1,0:T(8,128)} %str_in.1, f32[2,64,128]{2,1,0:T(8,128)} %wind_in.1, f32[2,64,128]{2,1,0:T(8,128)} %cur_in.1, f32[5,64,128]{2,1,0:T(8,128)} %area_in.1, ...), custom_call_target="tpu_custom_call" | custom-call | flops 29491200 | bytes 901120 | tf_op jit(solution)/shard_map/pallas_call | solution.py:582
  19.4 1.3 %shard_map.131 = (f32[1,10,256,128]{3,2,1,0:T(8,128)}, f32[2,64,128]{2,1,0:T(8,128)}, f32[3,64,128]{2,1,0:T(8,128)}) custom-call(f32[10,256,128]{2,1,0:T(8,128)S(1)} %get-tuple-element.10.strips, f32[2,64,128]{2,1,0:T(8,128)S(1)} %get-tuple-element.11.vel, f32[3,64,128]{2,1,0:T(8,128)S(1)} %get-tuple-element.12.stress, s32[1,8]{1,0:T(1,128)S(1)} %get-tuple-element.13.writer), custom_call_target="tpu_custom_call" | custom-call | tf_op jit(solution)/shard_map/pallas_call | solution.py:624

commit v3 on v2

--- a/solution.py
+++ b/solution.py
@@ -171,7 +171,39 @@
         for at in (0, PAD + rows):
             main[f, at : at + 8, :] = zero
             side[f, at : at + 8, :] = zero
-    for copy in arriving:
+    arriving[0].wait()
+    arriving[1].wait()
+
+    peers = 3 + len(others) + 3 * not_top.astype(jnp.int32) + 3 * above_bottom.astype(jnp.int32)
+    peers = peers + is_top.astype(jnp.int32)
+    peers = peers + other_e.astype(jnp.int32) + other_w.astype(jnp.int32)
+    pl.semaphore_wait(barrier, peers)
+
+    def remote(src, dst, send, recv, row, col):
+        return pltpu.make_async_remote_copy(
+            src_ref=src,
+            dst_ref=dst,
+            send_sem=send,
+            recv_sem=recv,
+            device_id={"row": row, "col": col},
+            device_id_type=pl.DeviceIdType.MESH,
+        )
+
+    crossing = [
+        remote(
+            strips.at[n, own, :],
+            strips.at[n, own, :],
+            x_send.at[n * len(others) + k],
+            x_recv.at[n * len(others) + k],
+            other,
+            c,
+        )
+        for n in range(2 * cats)
+        for k, other in enumerate(others)
+    ]
+    for copy in crossing[: len(others)]:
+        copy.start()
+    for copy in arriving[2:]:
         copy.wait()
     expand_into(ocean_ref, land_ref)
     expand_into(icy_ref, ice_ref)
@@ -235,21 +267,6 @@
             pack_e[g, here, :] = packed_e
             pack_w[g, here, :] = packed_w
 
-    peers = 3 + len(others) + 3 * not_top.astype(jnp.int32) + 3 * above_bottom.astype(jnp.int32)
-    peers = peers + is_top.astype(jnp.int32)
-    peers = peers + other_e.astype(jnp.int32) + other_w.astype(jnp.int32)
-    pl.semaphore_wait(barrier, peers)
-
-    def remote(src, dst, send, recv, row, col):
-        return pltpu.make_async_remote_copy(
-            src_ref=src,
-            dst_ref=dst,
-            send_sem=send,
-            recv_sem=recv,
-            device_id={"row": row, "col": col},
-            device_id_type=pl.DeviceIdType.MESH,
-        )
-
     mid = slice(hr, hr + height)
     low = slice(0, hr)
     high = slice(hr + height, rows)
@@ -316,35 +333,12 @@
         for copy in down:
             copy.start()
 
-    crossing = []
-    for k, other in enumerate(others):
-        for part, ref in enumerate((area_own, vol_own)):
-            crossing.append(
-                remote(
-                    ref,
-                    ref,
-                    x_send.at[2 * k + part],
-                    x_recv.at[2 * k + part],
-                    other,
-                    c,
-                )
-            )
-    for copy in crossing:
+    for copy in crossing[len(others) :]:
         copy.start()
-    forwards = []
-    for part, ref in enumerate((area_own, vol_own)):
-        forwards.append(
-            remote(
-                ref,
-                ref,
-                f_send.at[part],
-                f_recv.at[part],
-                partner,
-                c,
-            )
-        )
-    for copy in forwards:
-        copy.start()
+    forward = remote(
+        strips.at[:, own, :], strips.at[:, own, :], f_send.at[0], f_recv.at[0], partner, c
+    )
+    forward.start()
 
     @pl.when(r == 0)
     def _():
@@ -418,8 +412,8 @@
     last_own = first + height - 1
     last_north = PAD + rows - 1
 
-    def cycle(_, carry):
-        for k in range(rows // 8):
+    def cycle(low_chunk):
+        for k in range(low_chunk, rows // 8):
             here = slice(PAD + 8 * k, PAD + 8 * k + 8)
             south = slice(PAD + 8 * k - 1, PAD + 8 * k + 7)
             us, ud, vs, vd = [], [], [], []
@@ -458,7 +452,7 @@
                 line = 3 * i + f
                 t[2 + f, last_north + 1 : last_north + 2, :] = own_edge[line : line + 1, :]
 
-        for k in range(rows // 8):
+        for k in range(low_chunk, rows // 8):
             here = slice(PAD + 8 * k, PAD + 8 * k + 8)
             north = slice(PAD + 8 * k + 1, PAD + 8 * k + 9)
             p, d, q, e = [], [], [], []
@@ -490,24 +484,47 @@
                 ca, cb = t[7, here, :], t[8, here, :]
                 t[0, here, :] = ca * rx + cb * ry + t[5, here, :]
                 t[1, here, :] = ca * ry - cb * rx + t[6, here, :]
+
+    def relays(n):
+        copies = []
+        for k in range(len(others)):
+            source = lax.rem(r + nr - 2 * (k + 1), nr)
+            lines = pl.ds(pl.multiple_of(source * height, height), height)
+            block = strips.at[n, lines, :]
+            slot = n * len(others) + k
+            copies.append(
+                remote(block, block, f_send.at[1 + slot], f_recv.at[1 + slot], partner, c)
+            )
+        return copies
+
+    def relay(fields):
+        for n in fields:
+            for k, copy in enumerate(relays(n)):
+                crossing[n * len(others) + k].wait_recv()
+                copy.start()
+
+    early = SUB - 8 - 1
+    count = 2 * cats
+
+    def early_cycle(i, carry):
+        cycle(0)
         return carry
 
-    early = SUB * 3 // 4
-    lax.fori_loop(0, early, cycle, 0)
-
-    relays = []
-    for k in range(len(others)):
-        source = lax.rem(r + nr - 2 * (k + 1), nr)
-        lines = pl.ds(pl.multiple_of(source * height, height), height)
-        for part in range(2):
-            crossing[2 * k + part].wait_recv()
-            block = strips.at[part * cats : (part + 1) * cats, lines, :]
-            slot = 2 + 2 * k + part
-            copy = remote(block, block, f_send.at[slot], f_recv.at[slot], partner, c)
-            copy.start()
-            relays.append(copy)
-
-    lax.fori_loop(0, SUB - early, cycle, 0)
+    def late_cycle(i, carry):
+        @pl.when(i == SUB // 2)
+        def _():
+            relay(range(0, count // 2))
+
+        @pl.when(i == SUB * 3 // 4)
+        def _():
+            relay(range(count // 2, count * 4 // 5))
+
+        cycle((hr - 8) // 8)
+        return carry
+
+    lax.fori_loop(0, early, early_cycle, 0)
+    lax.fori_loop(early, SUB, late_cycle, 0)
+    relay(range(count * 4 // 5, count))
 
     inner = slice(first, first + height)
     for f in range(2):
@@ -517,8 +534,10 @@
 
     for copy in crossing:
         copy.wait_send()
-    for copy in forwards + relays:
-        copy.wait()
+    forward.wait()
+    for n in range(count):
+        for copy in relays(n):
+            copy.wait()
 
 
 def place(strips, vel, stress, writer, restart_out, vel_out, str_out, blank, sem):
@@ -570,7 +589,7 @@
     groups = -(-FIELDS // (breadth // LANES))
     vmem = pl.BlockSpec(memory_space=pltpu.VMEM)
     hbm = pl.BlockSpec(memory_space=pltpu.HBM)
-    relayed = max(2 * (nr // 2 - 1), 1)
+    relayed = max(2 * cats * (nr // 2 - 1), 1)
     f32 = jnp.float32
     land, ice = land.T, ice.T
     writer = writer[None]
@@ -610,8 +629,8 @@
             pltpu.SemaphoreType.DMA((8,)),
             pltpu.SemaphoreType.DMA((relayed,)),
             pltpu.SemaphoreType.DMA((relayed,)),
-            pltpu.SemaphoreType.DMA((2 + relayed,)),
-            pltpu.SemaphoreType.DMA((2 + relayed,)),
+            pltpu.SemaphoreType.DMA((1 + relayed,)),
+            pltpu.SemaphoreType.DMA((1 + relayed,)),
             pltpu.SemaphoreType.DMA((11,)),
         ],
         compiler_params=pltpu.CompilerParams(

time: 20.8 us -> 21.6 us (1.038)
  Pallas kernels: 20 us -> 20.8 us
    pallas_call x1, Pallas kernels: 18.7 us -> 19.5 us  [shards(): pl.pallas_call(functools.partial(kernel, nr, nc), out_shape=(jax.ShapeDty...]
where the time goes in v3:
time: 21.6 us; the launch traced here: 21.4 us
  Pallas kernels  20.8 us (96%)
  between operations  0.64 us (3%)
    pallas_call x1, Pallas kernels, shards(): pl.pallas_call(functools.partial(kernel, nr, nc), out_shape=(jax.ShapeDty...  19.5 us
    pallas_call x1, Pallas kernels, shards(): pl.pallas_call(place, out_shape=(jax.ShapeDtypeStruct((1,) + strips.shape...  1.31 us

profile of v3, /device:TPU:0, one launch (start us, length us, event | category | flops | bytes accessed | tf_op | source)
XLA Modules:
  0.0 21.4 jit_solution(16048507001665143904)
XLA Ops:
  0.6 19.5 %shard_map.130 = (f32[2,64,128]{2,1,0:T(8,128)S(1)}, f32[3,64,128]{2,1,0:T(8,128)S(1)}, f32[10,256,128]{2,1,0:T(8,128)S(1)}, s32[1,8]{1,0:T(1,128)S(1)}) custom-call(f32[2,64,128]{2,1,0:T(8,128)} %vel_in.1, f32[3,64,128]{2,1,0:T(8,128)} %str_in.1, f32[2,64,128]{2,1,0:T(8,128)} %wind_in.1, f32[2,64,128]{2,1,0:T(8,128)} %cur_in.1, f32[5,64,128]{2,1,0:T(8,128)} %area_in.1, ...), custom_call_target="tpu_custom_call" | custom-call | flops 29491200 | bytes 901120 | tf_op jit(solution)/shard_map/pallas_call | solution.py:601
  20.1 1.3 %shard_map.131 = (f32[1,10,256,128]{3,2,1,0:T(8,128)}, f32[2,64,128]{2,1,0:T(8,128)}, f32[3,64,128]{2,1,0:T(8,128)}) custom-call(f32[10,256,128]{2,1,0:T(8,128)S(1)} %get-tuple-element.10.strips, f32[2,64,128]{2,1,0:T(8,128)S(1)} %get-tuple-element.11.vel, f32[3,64,128]{2,1,0:T(8,128)S(1)} %get-tuple-element.12.stress, s32[1,8]{1,0:T(1,128)S(1)} %get-tuple-element.13.writer), custom_call_target="tpu_custom_call" | custom-call | tf_op jit(solution)/shard_map/pallas_call | solution.py:643
